TPU v7x, 32 devices: a whole 2x2x4 slice. The times are simulated.
32 devices in a mesh: seq: 4 (over x, core), level: 8 (over z, y).
Axes of the slice: x: 2, y: 2, z: 4, core: 2. Of those that a mesh axis runs over, the one named last changes fastest.
Arguments:
- states: float32 [32, 480, 64, 128], P('seq', 'level'), may hold values from -0.3 to 0.3
- xbc: bfloat16 [32, 8, 1792], P('seq', None, 'level'), may hold values from -1.796875 to 1.796875
- rates: float32 [32, 8, 24], P('seq'), may hold values from 0.02 to 0.8
- level_weights: float32 [32, 8, 480], P('seq', None, 'level'), may hold values from 0.1 to 1
- positions: int32 [32], P('seq'), may hold values from 0 to 1048567, as said below
- accepted: int32 [32], P('seq'), may hold values from 0 to 8
Outputs:
- outputs: bfloat16 [32, 8, 1536], P('seq', None, 'level')
- new_states: float32 [32, 480, 64, 128], P('seq', 'level')
- acceptance: float32 [], replicated
Inputs may be any that keep to these rules, and one draw needn't show every extreme that they name: `positions`: p + 8 stays below 2**20.
All inputs are finite; a program needn't handle non-finite values.
Results may differ from a plain program's by a relative error of at most 0.0019.
Values may be sent and summed in bfloat16 or wider, within the bound.
No kernel may reach another device: no remote copies, remote signals or barrier semaphores. Data moves between devices by JAX's collectives and lax.ppermute only.
A program may use at most 128 MiB of HBM per device.

v0:
```python
import jax
import jax.numpy as jnp
from jax import lax
from jax.sharding import PartitionSpec as P

H = 24
P_SIZE = 64
N = 128
L = 20
K = 8


def passed_along(x, axis, by):
    devices = lax.axis_size(axis)
    return lax.ppermute(x, axis, [(i, (i + by) % devices) for i in range(devices)])


def on_device(states, xbc, rates, level_weights, positions, accepted):
    highest = lax.Precision.HIGHEST
    seqs_local, local_count, width_p, width_n = states.shape
    offset = L // 2
    total_entries = H * L
    gathered = lax.all_gather(xbc, "level", axis=2, tiled=True).astype(jnp.float32)
    values = gathered[:, :, : H * P_SIZE].reshape(seqs_local, K, H, P_SIZE)
    in_vecs = gathered[:, :, H * P_SIZE : H * P_SIZE + N]
    out_vecs = gathered[:, :, H * P_SIZE + N :]
    cumul = jnp.cumsum(-rates, axis=1)
    first_entry = lax.axis_index("level") * local_count
    entries = first_entry + jnp.arange(local_count, dtype=jnp.int32)
    global_ids = (entries + offset) % total_entries
    head_of = global_ids // L
    level_of = global_ids % L
    head_ids = jnp.arange(H, dtype=jnp.int32)
    select = (head_of[:, None] == head_ids[None, :]).astype(jnp.float32)
    occupied = (jnp.right_shift(positions[:, None], level_of[None, :]) % 2).astype(jnp.float32)
    cum_local = jnp.einsum("sth,jh->stj", cumul, select, precision=highest)
    readout = jnp.einsum("sjpn,stn->stjp", states, out_vecs, precision=highest)
    factor = level_weights * occupied[:, None, :] * jnp.exp(cum_local)
    steps_all = jnp.arange(K, dtype=jnp.int32)
    causal = steps_all[None, :] <= steps_all[:, None]
    scores = jnp.einsum("stn,sun->stu", out_vecs, in_vecs, precision=highest)
    spread = cumul[:, :, None, :] - cumul[:, None, :, :]
    mixing = (
        jnp.where(causal[None, :, :, None], jnp.exp(jnp.minimum(spread, 0.0)), 0.0)
        * scores[..., None]
    )
    is_first = (level_of == 0).astype(jnp.float32)
    devices = lax.axis_size("level")
    own_width = H * P_SIZE // devices
    most_heads = 1
    distances = []
    for sender in range(devices):
        start_global = (sender * local_count + offset) % total_entries
        head_low = start_global // L
        head_count = (start_global + local_count - 1) // L - head_low + 1
        most_heads = max(most_heads, head_count)
        for slot_index in range(head_count):
            head_now = (head_low + slot_index) % H
            for receiver in range(
                head_now * P_SIZE // own_width, ((head_now + 1) * P_SIZE - 1) // own_width + 1
            ):
                gap = (receiver - sender) % devices
                if gap > devices // 2:
                    gap = gap - devices
                if gap != 0 and gap not in distances:
                    distances.append(gap)
    first_head = (first_entry + offset) % total_entries // L
    slot_heads = (first_head + jnp.arange(most_heads, dtype=jnp.int32)) % H
    select_slot = (head_of[:, None] == slot_heads[None, :]).astype(jnp.float32)
    pick_head = (head_ids[:, None] == slot_heads[None, :]).astype(jnp.float32)
    states_slot = jnp.einsum("stj,stjp,ji->stip", factor, readout, select_slot, precision=highest)
    weight_slot = jnp.einsum(
        "stj,ji->sti", level_weights, select_slot * is_first[:, None], precision=highest
    )
    mixing_slot = jnp.einsum("stuh,hi->stui", mixing, pick_head, precision=highest)
    values_slot = jnp.einsum("suhp,hi->suip", values, pick_head, precision=highest)
    drafts_slot = weight_slot[..., None] * jnp.einsum(
        "stui,suip->stip", mixing_slot, values_slot, precision=highest
    )
    flat_slot = (states_slot + drafts_slot).reshape(seqs_local, K, most_heads * P_SIZE)

    def toward(distance):
        receiver_now = (lax.axis_index("level") + distance) % devices
        feature_ids = receiver_now * own_width + jnp.arange(own_width, dtype=jnp.int32)
        slot_of = (feature_ids // P_SIZE - first_head) % H
        valid = (slot_of < most_heads).astype(jnp.float32)
        offsets = jnp.clip(slot_of * P_SIZE + feature_ids % P_SIZE, 0, most_heads * P_SIZE - 1)
        picked = jnp.take(flat_slot, offsets, axis=2)
        return picked * valid[None, None, :]

    summed = toward(0)
    for distance in distances:
        summed = summed + passed_along(toward(distance), "level", distance)
    outputs = summed.astype(jnp.bfloat16)
    new_position = positions + accepted
    levels_all = jnp.arange(L, dtype=jnp.int32)
    changed = jnp.bitwise_xor(positions, new_position)
    top_level = (
        jnp.sum(
            (jnp.right_shift(changed[:, None], levels_all[None, :]) > 0).astype(jnp.int32), axis=1
        )
        - 1
    )
    staying = occupied * (level_of[None, :] > top_level[:, None]).astype(jnp.float32)
    leaving = occupied * (level_of[None, :] < top_level[:, None]).astype(jnp.float32)
    target = (level_of[None, :] == top_level[:, None]).astype(jnp.float32)
    reach = min(devices - 1, (L - 2 + local_count) // local_count)
    same_head = (head_of[:, None] == head_of[None, :]).astype(jnp.float32)
    incoming = jnp.einsum("ab,sb,sbpn->sapn", same_head, leaving, states, precision=highest)
    place = target * (head_of == first_head).astype(jnp.float32)[None, :]
    for distance in range(1, reach + 1):
        receiver_start = (first_entry + distance * local_count + offset) % total_entries
        receiver_head = receiver_start // L
        target_global = receiver_head * L + top_level
        in_range = (
            (target_global >= receiver_start) & (target_global < receiver_start + local_count)
        ).astype(jnp.float32)
        pick_mask = (
            leaving * (head_of == receiver_head).astype(jnp.float32)[None, :] * in_range[:, None]
        )
        folded_sum = jnp.einsum("sj,sjpn->spn", pick_mask, states, precision=highest)
        received = passed_along(folded_sum.astype(jnp.bfloat16), "level", distance).astype(
            folded_sum.dtype
        )
        incoming = incoming + place[:, :, None, None] * received[:, None]
    merged = staying[:, :, None, None] * states + target[:, :, None, None] * incoming
    new_occ = (jnp.right_shift(new_position[:, None], level_of[None, :]) % 2).astype(jnp.float32)
    live = (steps_all[None, :] < accepted[:, None]).astype(jnp.float32)
    cum_taken = jnp.sum(-rates * live[:, :, None], axis=1)
    taken_local = jnp.einsum("sh,jh->sj", cum_taken, select, precision=highest)
    token_pos = positions[:, None] + steps_all[None, :]
    start_new = jnp.left_shift(
        jnp.right_shift(new_position[:, None], level_of[None, :] + 1), level_of[None, :] + 1
    )
    level_span = jnp.left_shift(jnp.int32(1), level_of)
    inside = (
        (token_pos[:, None, :] >= start_new[:, :, None])
        & (token_pos[:, None, :] < start_new[:, :, None] + level_span[None, :, None])
    ).astype(jnp.float32) * live[:, None, :]
    token_decay = jnp.exp(jnp.minimum(taken_local[:, None, :] - cum_local, 0.0)) * live[:, :, None]
    values_local = jnp.einsum("suhp,jh->sujp", values, select, precision=highest)
    tokens = jnp.einsum(
        "sju,suj,sujp,sun->sjpn", inside, token_decay, values_local, in_vecs, precision=highest
    )
    new_states = new_occ[:, :, None, None] * (
        jnp.exp(taken_local)[:, :, None, None] * merged + tokens
    )
    total_taken = lax.psum(jnp.sum(accepted.astype(jnp.float32)), "seq")
    acceptance = total_taken / (lax.axis_size("seq") * seqs_local * K)
    return (outputs, new_states, acceptance)


def solution(mesh):
    in_specs = (
        P("seq", "level", None, None),
        P("seq", None, "level"),
        P("seq", None, None),
        P("seq", None, "level"),
        P("seq"),
        P("seq"),
    )
    out_specs = (P("seq", None, "level"), P("seq", "level", None, None), P())
    return jax.shard_map(
        on_device, mesh=mesh, in_specs=in_specs, out_specs=out_specs, check_vma=False
    )
```

profile of v0, /device:TPU:0, one launch (start us, length us, event | category | flops | bytes accessed | tf_op | source)
XLA Modules:
  0.0 248.4 jit_solution(6325862648210588140)
XLA Ops:
  0.6 0.6 iota_compare_fusion.3
  1.2 1.0 copy.66
  2.3 75.7 %all_gather.3 = bf16[8,8,1792]{1,0,2:T(8,128)(2,1)S(1)} all-gather(bf16[8,8,224]{1,0,2:T(8,128)(2,1)S(1)} %copy.66), channel_id=1, replica_groups=mesh['seq'=4,'level'=8] {'level'}, dimensions={2}, use_global_device_ids=true | all-gather | bytes 258048 | tf_op jit(solution)/shard_map/all_gather | solution.py:23
  77.9 0.7 fusion.77
  78.7 0.2 slice.17
  79.0 0.6 and_select_fusion.6
  79.5 0.5 broadcast_add_fusion.2
  80.1 0.7 fusion.58
  80.8 1.2 fusion.76
  82.0 1.3 iota_add_fusion
  83.3 0.6 compare_select_fusion.1
  83.9 0.6 compare_and_fusion
  84.6 1.1 copy.96
  85.9 22.7 %fusion.41 = f32[8,8,60,64]{3,1,2,0:T(8,128)} fusion(f32[8,60,64,128]{3,2,1,0:T(8,128)} %param.8, bf16[8,8,128]{2,1,0:T(8,128)(2,1)S(1)} %copy.96), kind=kOutput, calls=%fused_computation.48 | convolution fusion | flops 377487360 | bytes 16728064 | tf_op jit(solution)/shard_map/sjpn,stn->stjp/dot_general | solution.py:37
  108.5 0.7 fusion.81
  109.3 2.4 copy.93
  111.8 0.2 convolution_bitcast_fusion
  112.1 1.3 convolution_bitcast_fusion.1
  113.5 0.9 multiply_reduce_fusion
  114.6 2.7 %fusion.14 = f32[8,8,8,4]{2,3,1,0:T(4,128)S(1)} fusion(f32[8,8,8]{2,1,0:T(8,128)} %fusion.81, f32[8,8,24]{2,1,0:T(8,128)S(1)} %reduce_window_sum.11, pred[8,8]{1,0:T(8,128)(4,1)} %iota_compare_fusion.3, s32[4]{0:T(128)S(1)} %and_select_fusion.7), kind=kOutput, calls=%fused_computation.19 | convolution fusion | flops 639072 | bytes 16464 | tf_op jit(solution)/shard_map/stuh,hi->stui/dot_general | solution.py:75
  117.2 0.3 fusion.20
  117.6 0.8 fusion.55
  118.4 0.9 bitcast_multiply_fusion.4
  119.3 3.5 %fusion.11 = f32[8,8,4,64]{3,2,1,0:T(4,128)S(1)} fusion(f32[8,8,60,64]{3,1,2,0:T(8,128)} %fusion.41, f32[8,4,64,8]{2,3,1,0:T(8,128)S(1)} %fusion.20, f32[8,8,4]{2,1,0:T(8,128)S(1)} %copy.69, f32[60,8,8]{0,2,1:T(8,128)S(1)} %get-tuple-element.24, f32[60,4]{0,1:T(4,128)S(1)} %compare_convert_fusion.1), kind=kOutput, calls=%fused_computation.17 | convolution fusion | flops 11844608 | bytes 1131456 | tf_op jit(solution)/shard_map/stj,stjp,ji->stip/dot_general | solution.py:71
  122.8 0.4 copy.95
  123.2 0.7 pad_clamp_fusion
  123.8 0.9 gather_fusion.1
  124.8 0.3 copy.78
  125.1 1.3 bitcast_multiply_fusion.2
  126.7 0.8 convert_reduce_fusion
  127.5 1.3 compare_select_fusion.3
  128.9 21.6 %fusion.7 = f32[8,1,64,128]{3,1,2,0:T(1,128)S(1)} fusion(f32[8,60,1,1]{1,2,3,0:T(1,128)S(1)} %bitcast.91, f32[8,60,64,128]{3,2,1,0:T(8,128)} %param.8), kind=kOutput, calls=%fused_computation.10 | convolution fusion | flops 47185920 | bytes 15992704 | tf_op jit(solution)/shard_map/sj,sjpn->spn/dot_general | solution.py:121
  150.5 0.7 convert_element_type.113
  151.2 1.4 collective-permute-start.1
  152.6 0.7 compare_convert_fusion
  153.2 0.6 convert_reduce_fusion.1
  153.9 0.6 pad_clamp_fusion.1
  154.5 2.0 bitcast_multiply_fusion
  156.4 2.1 copy.90
  158.5 16.5 %fusion.39 = f32[8,60,64,128]{3,1,2,0:T(8,128)} fusion(f32[8,8,60,64]{2,1,3,0:T(8,128)S(1)} %copy.90, bf16[8,8,128]{2,1,0:T(8,128)(2,1)} %copy-done.1), kind=kOutput, calls=%fused_computation.46 | convolution fusion | flops 377487360 | bytes 16728064 | tf_op jit(solution)/shard_map/sju,suj,sujp,sun->sjpn/dot_general | solution.py:142
  175.0 11.1 %broadcast_multiply_fusion = f32[8,60,64,128]{3,2,1,0:T(8,128)} fusion(f32[8,60,64,128]{3,2,1,0:T(8,128)} %param.8, f32[8,60]{1,0:T(8,128)} %get-tuple-element.27), kind=kLoop, calls=%fused_computation.12 | loop fusion | flops 3932160 | bytes 31459200 | tf_op jit(solution)/shard_map/ab,sb,sbpn->sapn/dot_general | solution.py:109
  186.2 6.8 %psum.7 = f32[]{:T(128)} all-reduce(f32[]{:T(128)} %convert_reduce_fusion.1), channel_id=1, replica_groups=mesh['seq'=4,'level'=8] {'seq'}, use_global_device_ids=true, to_apply=%region_4.6 | all-reduce | flops 1 | bytes 8 | tf_op jit(solution)/shard_map/psum | solution.py:148
  193.0 1.0 gather_fusion
  194.1 0.3 copy.76
  195.1 1.5 fusion.30
  196.6 0.9 convert_element_type.114
  197.5 38.7 %fusion.4 = f32[8,60,64,128]{3,1,2,0:T(8,128)S(1)} fusion(f32[8,60,64,128]{3,1,2,0:T(8,128)} %fusion.39, f32[8,60,64,128]{3,2,1,0:T(8,128)} %param.8, f32[8,64,128]{2,1,0:T(8,128)S(1)} %convert_element_type.114, f32[8,60]{1,0:T(8,128)S(1)} %get-tuple-element.30, f32[8,60]{1,0:T(8,128)S(1)} %copy-done, f32[8,60]{1,0:T(8,128)S(1)} %get-tuple-element.29, ...), kind=kOutput, calls=%fused_computation.7 | convolution fusion | flops 2862616064 | bytes 63186544 | tf_op jit(solution)/shard_map/ab,sb,sbpn->sapn/dot_general | solution.py:109
  236.2 11.1 %copy.83 = f32[8,60,64,128]{3,2,1,0:T(8,128)} copy(f32[8,60,64,128]{3,1,2,0:T(8,128)S(1)} %fusion.4) | data formatting | bytes 31457280
  (30 shorter events, 1.0 us)
Async XLA Ops:
  79.0 48.5 %copy-start.2 = (s32[60]{0:T(128)}, s32[60]{0:T(128)S(1)}, u32[]{:S(2)}) copy-start(s32[60]{0:T(128)S(1)} %and_select_fusion.8) | copy-start | bytes 724
  85.9 23.4 %copy-start.1 = (bf16[8,8,128]{2,1,0:T(8,128)(2,1)}, bf16[8,8,128]{2,1,0:T(8,128)(2,1)S(1)}, u32[]{:S(2)}) copy-start(bf16[8,8,128]{2,1,0:T(8,128)(2,1)S(1)} %copy.97) | copy-start | bytes 49156
  111.7 40.9 %copy-start.5 = (s32[60]{0:T(128)S(1)}, s32[60]{0:T(128)}, u32[]{:S(2)}) copy-start(s32[60]{0:T(128)} %get-tuple-element.41) | copy-start | bytes 724
  111.7 41.5 %copy-start.6 = (s32[8]{0:T(128)S(1)}, s32[8]{0:T(128)}, u32[]{:S(2)}) copy-start(s32[8]{0:T(128)} %param.13) | copy-start | bytes 100
  126.4 68.7 %collective-permute-start = (f32[8,8,192]{2,1,0:T(8,128)}, f32[8,8,192]{2,1,0:T(8,128)}, u32[]{:S(2)}, u32[]{:S(2)}) collective-permute-start(f32[8,8,192]{2,1,0:T(8,128)} %bitcast_multiply_fusion.2), channel_id=1, source_target_pairs={{0,1},{1,2},{2,3},{3,4},{4,5},{5,6},{6,7},{7,0},{8,9},{9,10},{10,1... | collective-permute-start | bytes 147464 | tf_op jit(solution)/shard_map/ppermute | solution.py:15
  127.5 26.9 %copy-start.3 = (s32[60]{0:T(128)S(1)}, s32[60]{0:T(128)}, u32[]{:S(2)}) copy-start(s32[60]{0:T(128)} %copy-done.2) | copy-start | bytes 724
  151.2 45.4 %collective-permute-start.1 = (bf16[8,64,128]{2,1,0:T(8,128)(2,1)}, bf16[8,64,128]{2,1,0:T(8,128)(2,1)}, u32[]{:S(2)}, u32[]{:S(2)}) collective-permute-start(bf16[8,64,128]{2,1,0:T(8,128)(2,1)} %convert_element_type.113), channel_id=1, source_target_pairs={{0,1},{1,2},{2,3},{3,4},{4,5},{5,6},{6,7},{7,0},{8,9},{9,10},{10,1... | collective-permute-start | bytes 393224 | tf_op jit(solution)/shard_map/ppermute | solution.py:15
  175.0 22.5 %copy-start = (f32[8,60]{1,0:T(8,128)S(1)}, f32[8,60]{1,0:T(8,128)}, u32[]{:S(2)}) copy-start(f32[8,60]{1,0:T(8,128)} %compare_convert_fusion) | copy-start | bytes 5764
  175.0 22.5 %copy-start.4 = (s32[60]{0:T(128)S(1)}, s32[60]{0:T(128)}, u32[]{:S(2)}) copy-start(s32[60]{0:T(128)} %copy-done.2) | copy-start | bytes 724
where the time goes:
time: 249 us; the launch traced here: 248 us
  matrix products  111 us (45%)
  blocking collectives  82.5 us (33%)
  other arithmetic  28.3 us (11%)
  local copies, waits for them, and re-layouts  22.1 us (9%)
  between operations  2.68 us (1%)
    all_gather x1, blocking collectives, on_device(): lax.all_gather(xbc, 'level', axis=2, tiled=True).astype(jnp.float32)  75.7 us
    dot_general x1, matrix products, on_device(): jnp.einsum('ab,sb,sbpn->sapn', same_head, leaving, states, precision=high...  38.7 us
    dot_general x1, matrix products, on_device(): readout = jnp.einsum('sjpn,stn->stjp', states, out_vecs, precision=highest)  22.7 us
    dot_general x1, matrix products, on_device(): jnp.einsum('sj,sjpn->spn', pick_mask, states, precision=highest)  21.6 us
    dot_general x1, matrix products, on_device(): jnp.einsum('sju,suj,sujp,sun->sjpn', inside, token_decay, values_local, i...  16.5 us
    unnamed x18, local copies, waits for them, and re-layouts  13.4 us
    dot_general x1, other arithmetic, on_device(): jnp.einsum('ab,sb,sbpn->sapn', same_head, leaving, states, precision=high...  11.1 us
    psum x1, blocking collectives, on_device(): total_taken = lax.psum(jnp.sum(accepted.astype(jnp.float32)), 'seq')  6.84 us
  transfers between devices with their start and end apart: 2, of which 0 were waited for; matrix products, arithmetic and copies ran while one was open for 25% of the time, Pallas kernels for 0%

commit v1 on v0

--- a/solution.py
+++ b/solution.py
@@ -1,6 +1,10 @@
+import functools
+
 import jax
 import jax.numpy as jnp
 from jax import lax
+from jax.experimental import pallas as pl
+from jax.experimental.pallas import tpu as pltpu
 from jax.sharding import PartitionSpec as P
 
 H = 24
@@ -8,6 +12,7 @@
 N = 128
 L = 20
 K = 8
+VMEM = 24 * 2**20
 
 
 def passed_along(x, axis, by):
@@ -150,6 +155,365 @@
     return (outputs, new_states, acceptance)
 
 
+def highest_bit(value):
+    return sum((jnp.right_shift(value, bit) > 0).astype(jnp.int32) for bit in range(L)) - 1
+
+
+def split(value):
+    high = value.astype(jnp.bfloat16)
+    low = (value - high.astype(jnp.float32)).astype(jnp.bfloat16)
+    return high, low
+
+
+def dot_nt(left, right):
+    return lax.dot_general(
+        left, right, (((1,), (1,)), ((), ())), preferred_element_type=jnp.float32
+    )
+
+
+def weighted_queries(factor, out_vecs):
+    high, low = split(factor * out_vecs)
+    rows = jnp.concatenate([high, low], axis=0)
+    return jnp.concatenate([rows, rows], axis=1)
+
+
+class Plan:
+    def __init__(self, devices, states, xbc, rates):
+        self.seqs, self.count, self.width_p, self.width_n = states.shape
+        self.steps = xbc.shape[1]
+        self.shard = xbc.shape[2]
+        self.heads = rates.shape[2]
+        self.devices = devices
+        self.offset = L // 2
+        self.own = self.count // L
+        self.slots = self.own + 1
+        self.rows = self.seqs * self.steps
+        self.low = (self.steps - 1).bit_length()
+        self.starts = [0] + [L - self.offset + i * L for i in range(self.own)] + [self.count]
+        self.value_width = self.heads * self.width_p
+
+    def fits(self):
+        return (
+            self.count % L == 0
+            and L - self.offset == self.offset
+            and self.devices & (self.devices - 1) == 0
+            and self.devices > 1
+            and self.heads == self.own * self.devices
+            and self.steps == 8
+            and self.low <= self.offset
+        )
+
+    def levels(self, slot):
+        first = self.offset if slot == 0 else 0
+        return [(j, first + j - self.starts[slot]) for j in range(self.starts[slot], self.starts[slot + 1])]
+
+
+def tables_kernel(plan, pos, acc, rates_ref, weights_ref, states_ref, factor_ref, taken_ref,
+                  decay_ref, mix_ref, fold_ref, count_ref):
+    rows, steps, seqs = plan.rows, plan.steps, plan.seqs
+    first_head = lax.axis_index("level") * plan.own
+    for s in range(seqs):
+        p, q = pos[s], pos[s] + acc[s]
+        top = highest_bit(jnp.bitwise_xor(p, q))
+        leaving = jnp.where(top >= plan.offset, p, 0)
+        total = None
+        for k in range(plan.offset):
+            bit = (jnp.right_shift(leaving, k) & 1) * (k < top).astype(jnp.int32)
+            term = states_ref[s, k] * bit.astype(jnp.float32)
+            total = term if total is None else total + term
+        fold_ref[s] = total.astype(fold_ref.dtype)
+    count_ref[...] = jnp.full(count_ref.shape, sum(acc[s] for s in range(seqs)).astype(jnp.float32))
+    rate = rates_ref[...].reshape(rows, plan.heads)
+    weight = weights_ref[...].reshape(rows, plan.count)
+    row = lax.broadcasted_iota(jnp.int32, (rows, rows), 0)
+    col = lax.broadcasted_iota(jnp.int32, (rows, rows), 1)
+    same = row // steps == col // steps
+    tri = same & (col <= row)
+    row1 = lax.broadcasted_iota(jnp.int32, (rows, 1), 0)
+    taken1 = jnp.zeros((rows, 1), jnp.int32)
+    place1 = jnp.zeros((rows, 1), jnp.int32)
+    for s in range(seqs):
+        taken1 = jnp.where(row1 // steps == s, acc[s], taken1)
+        place1 = jnp.where(row1 // steps == s, pos[s], place1)
+    live = same & (col % steps < taken1)
+    highest = lax.Precision.HIGHEST
+    cum = -jnp.dot(tri.astype(jnp.float32), rate, precision=highest, preferred_element_type=jnp.float32)
+    cum_taken = -jnp.dot(live.astype(jnp.float32), rate, precision=highest, preferred_element_type=jnp.float32)
+    grown = jnp.exp(cum)
+    grown_taken = jnp.exp(cum_taken)
+    token = jnp.exp(jnp.minimum(cum_taken - cum, 0.0)) * (row1 % steps < taken1).astype(jnp.float32)
+    head_lane = lax.broadcasted_iota(jnp.int32, (rows, plan.heads), 1)
+    lane = lax.broadcasted_iota(jnp.int32, (rows, plan.count), 1)
+    scale = None
+    for i in range(plan.slots):
+        hot = head_lane == lax.rem(first_head + i, plan.heads)
+
+        def pick(values):
+            return jnp.sum(jnp.where(hot, values, 0.0), axis=1, keepdims=True)
+
+        taken_ref[i] = jnp.broadcast_to(pick(grown_taken), (rows, plan.width_n))
+        decay_ref[i] = jnp.broadcast_to(pick(token), (rows, plan.width_p))
+        wide = jnp.broadcast_to(pick(grown), (rows, plan.count))
+        scale = wide if i == 0 else jnp.where(lane >= plan.starts[i], wide, scale)
+        if i > 0:
+            here = pick(cum)
+            across = jnp.sum(jnp.where(row == col, here, 0.0), axis=0, keepdims=True)
+            first = plan.starts[i]
+            mix = jnp.where(tri, jnp.exp(jnp.minimum(here - across, 0.0)), 0.0)
+            mix_ref[i - 1] = mix * weight[:, first : first + 1]
+    occupied = jnp.right_shift(place1, (lane + plan.offset) % L) & 1
+    factor_ref[...] = weight * occupied.astype(jnp.float32) * scale
+
+
+def assemble_kernel(plan, pair_ref, *refs):
+    *far_refs, states_ref, factor_ref, decay_ref, mix_ref = refs[: plan.devices // 2 - 1 + 4]
+    in_ref, out_ref, token_ref, draft_ref, send_ref, all_ref = refs[plan.devices // 2 - 1 + 4 :]
+    rows, shard = plan.rows, plan.shard
+    me = lax.axis_index("level")
+    for half, ref in enumerate([pair_ref, *far_refs]):
+        for side in range(2):
+            source = jnp.bitwise_xor(me, 2 * half + side)
+            part = ref[side].astype(jnp.float32).reshape(rows, shard)
+            all_ref[source] = part.astype(jnp.bfloat16)
+
+    def features(first, width, pieces):
+        k = lax.broadcasted_iota(jnp.int32, (shard, width), 0)
+        c = lax.broadcasted_iota(jnp.int32, (shard, width), 1)
+        total = None
+        start = first // shard
+        for piece in range(pieces):
+            source = start + piece
+            hot = (k + source * shard == c + first).astype(jnp.float32).astype(jnp.bfloat16)
+            index = jnp.minimum(source, plan.devices - 1)
+            term = jnp.dot(all_ref[index], hot, preferred_element_type=jnp.float32)
+            total = term if total is None else total + term
+        return total
+
+    def pieces_of(width):
+        return (width + shard - 2) // shard + 1
+
+    in_vecs = features(plan.value_width, plan.width_n, pieces_of(plan.width_n))
+    out_vecs = features(plan.value_width + plan.width_n, plan.width_n, pieces_of(plan.width_n))
+    in_ref[...] = in_vecs
+    out_ref[...] = out_vecs
+    scores = dot_nt(out_vecs.astype(jnp.bfloat16), in_vecs.astype(jnp.bfloat16))
+    drafts = []
+    for i in range(plan.slots):
+        head = lax.rem(me * plan.own + i, plan.heads)
+        value = features(head * plan.width_p, plan.width_p, pieces_of(plan.width_p))
+        token_ref[:, i * plan.width_p : (i + 1) * plan.width_p] = value * decay_ref[i]
+        if i > 0:
+            high, low = split(mix_ref[i - 1] * scores)
+            value = value.astype(jnp.bfloat16)
+            drafts.append(
+                jnp.dot(high, value, preferred_element_type=jnp.float32)
+                + jnp.dot(low, value, preferred_element_type=jnp.float32)
+            )
+        else:
+            drafts.append(jnp.zeros((rows, plan.width_p), jnp.float32))
+    draft_ref[...] = jnp.concatenate(drafts[:-1], axis=1)
+    steps = plan.steps
+    for s in range(plan.seqs):
+        at = slice(s * steps, (s + 1) * steps)
+        query = out_vecs[at]
+        total = None
+        for k, (j, _) in enumerate(plan.levels(plan.own)):
+            left = weighted_queries(factor_ref[at, j : j + 1], query)
+            right = jnp.concatenate(split(states_ref[s, k]), axis=1)
+            term = dot_nt(left, right)
+            total = term if total is None else total + term
+        send_ref[at] = total[:steps] + total[steps:] + drafts[-1][at]
+
+
+def states_kernel(plan, pos, acc, states_ref, factor_ref, taken_ref, in_ref, out_ref, token_ref,
+                  draft_ref, fold_ref, new_ref, own_ref):
+    s = pl.program_id(0)
+    steps, width_p, width_n = plan.steps, plan.width_p, plan.width_n
+    p = pos[s]
+    a = acc[s]
+    q = p + a
+    top = highest_bit(jnp.bitwise_xor(p, q))
+    bound = jnp.maximum(top, 0)
+    below = jnp.left_shift(1, bound) - 1
+    upto = jnp.where(top < 0, 0, jnp.left_shift(2, bound) - 1)
+    staying = p & q & jnp.bitwise_not(upto)
+    leaving = jnp.where(top < 0, 0, p & below)
+    step = lax.broadcasted_iota(jnp.int32, (2 * steps, width_n), 0) % steps
+    in_vecs = in_ref[...]
+    in_twice = jnp.concatenate([in_vecs, in_vecs], axis=0)
+    groups = []
+    for g in range(plan.low + 1):
+        level = bound if g == plan.low else g
+        wanted = (jnp.right_shift(q, level) & 1) == 1
+        if g < plan.low:
+            wanted = wanted & (top != g)
+        start = jnp.left_shift(jnp.right_shift(q, level + 1), level + 1)
+        last = jnp.minimum(start + jnp.left_shift(1, level) - p, a)
+        last = jnp.where(wanted, last, 0)
+        inside = (step >= start - p) & (step < last)
+        groups.append(jnp.where(inside, in_twice, 0.0).astype(jnp.bfloat16))
+    spread = jnp.concatenate(split(token_ref[...]), axis=0)
+    added = lax.dot_general(
+        spread, jnp.concatenate(groups, axis=1), (((0,), (0,)), ((), ())),
+        preferred_element_type=jnp.float32,
+    )
+
+    def tokens(i, g):
+        return added[i * width_p : (i + 1) * width_p, g * width_n : (g + 1) * width_n]
+
+    query = out_ref[...]
+    for i in range(plan.slots):
+        grown = taken_ref[i, 0:1, :]
+        merged = None
+        total = None
+        for j, level in plan.levels(i):
+            state = states_ref[0, j]
+            kept = (jnp.right_shift(staying, level) & 1).astype(jnp.float32)
+            new = state * (grown * kept)
+            if level < plan.low:
+                new = new + tokens(i, level)
+            new_ref[0, j] = new
+            left = (jnp.right_shift(leaving, level) & 1).astype(jnp.float32)
+            term = state * left
+            merged = term if merged is None else merged + term
+            if i < plan.own:
+                rows = weighted_queries(factor_ref[:, j : j + 1], query)
+                term = dot_nt(rows, jnp.concatenate(split(state), axis=1))
+                total = term if total is None else total + term
+        if i < plan.own:
+            at = slice(i * width_p, (i + 1) * width_p)
+            own_ref[:, at] = total[:steps] + total[steps:] + draft_ref[:, at]
+        base = plan.starts[i] - (plan.offset if i == 0 else 0)
+        here = top >= 0
+        if i == 0:
+            here = top >= plan.offset
+            merged = merged + fold_ref[0].astype(jnp.float32)
+        if i == plan.own:
+            here = here & (top < plan.offset)
+
+        @pl.when(here)
+        def _():
+            new_ref[0, base + top] = merged * grown + tokens(i, plan.low)
+
+
+def finish_kernel(plan, own_ref, received_ref, out_ref):
+    width_p = plan.width_p
+    own = own_ref[...]
+    first = own[:, :width_p] + received_ref[...]
+    total = jnp.concatenate([first, own[:, width_p:]], axis=1)
+    out_ref[...] = total.reshape(out_ref.shape).astype(out_ref.dtype)
+
+
+def summed_over(x, axis):
+    devices = lax.axis_size(axis)
+    if devices & (devices - 1):
+        return lax.psum(x, axis)
+    by = 1
+    while by < devices:
+        x = x + lax.ppermute(x, axis, [(i, i ^ by) for i in range(devices)])
+        by *= 2
+    return x
+
+
+def whole(shape, index=None):
+    zeros = (0,) * len(shape)
+    return pl.BlockSpec(shape, lambda *_: index if index else zeros)
+
+
+def fast_on_device(plan, states, xbc, rates, level_weights, positions, accepted):
+    devices, seqs, steps, rows = plan.devices, plan.seqs, plan.steps, plan.rows
+    count, slots, own = plan.count, plan.slots, plan.own
+    width_p, width_n = plan.width_p, plan.width_n
+    f32 = jnp.float32
+    swap = lambda x, by: lax.ppermute(x, "level", [(i, i ^ by) for i in range(devices)])
+    boundary = ((seqs, plan.offset, width_p, width_n), (0, count // plan.offset - 1, 0, 0))
+    beside = swap(xbc, 1)
+    factor, taken, decay, mix, fold, counted = pl.pallas_call(
+        functools.partial(tables_kernel, plan),
+        grid_spec=pltpu.PrefetchScalarGridSpec(
+            num_scalar_prefetch=2, grid=(1,),
+            in_specs=[whole(rates.shape), whole(level_weights.shape), whole(*boundary)],
+            out_specs=[whole((rows, count)), whole((slots, rows, width_n)), whole((slots, rows, width_p)),
+                       whole((own, rows, rows)), whole((seqs, width_p, width_n)), whole((8, 128))],
+        ),
+        out_shape=[
+            jax.ShapeDtypeStruct((rows, count), f32),
+            jax.ShapeDtypeStruct((slots, rows, width_n), f32),
+            jax.ShapeDtypeStruct((slots, rows, width_p), f32),
+            jax.ShapeDtypeStruct((own, rows, rows), f32),
+            jax.ShapeDtypeStruct((seqs, width_p, width_n), jnp.bfloat16),
+            jax.ShapeDtypeStruct((8, 128), f32),
+        ],
+        compiler_params=pltpu.CompilerParams(vmem_limit_bytes=VMEM),
+        cost_estimate=pl.CostEstimate(flops=2_000_000, bytes_accessed=3_000_000, transcendentals=0),
+        name="tables",
+    )(positions, accepted, rates, level_weights, states)
+    pair = jnp.stack([xbc, beside])
+    far = [swap(pair, by) for by in range(2, devices, 2)]
+    fold_in = passed_along(fold, "level", 1)
+    in_vecs, out_vecs, token, draft, send = pl.pallas_call(
+        functools.partial(assemble_kernel, plan),
+        grid=(1,),
+        in_specs=[whole(pair.shape)] * (1 + len(far)) + [
+            whole(*boundary), whole(factor.shape), whole(decay.shape), whole(mix.shape)],
+        out_specs=[whole((rows, width_n))] * 2 + [whole((rows, slots * width_p)), whole((rows, own * width_p)),
+                                                  whole((rows, width_p))],
+        out_shape=[jax.ShapeDtypeStruct((rows, width_n), f32)] * 2 + [
+            jax.ShapeDtypeStruct((rows, slots * width_p), f32),
+            jax.ShapeDtypeStruct((rows, own * width_p), f32),
+            jax.ShapeDtypeStruct((rows, width_p), f32)],
+        scratch_shapes=[pltpu.VMEM((devices, rows, plan.shard), jnp.bfloat16)],
+        compiler_params=pltpu.CompilerParams(vmem_limit_bytes=VMEM),
+        cost_estimate=pl.CostEstimate(flops=2_000_000, bytes_accessed=3_000_000, transcendentals=0),
+        name="assemble",
+    )(pair, *far, states, factor, decay, mix)
+    received = passed_along(send, "level", 1)
+    new_states, own_out = pl.pallas_call(
+        functools.partial(states_kernel, plan),
+        grid_spec=pltpu.PrefetchScalarGridSpec(
+            num_scalar_prefetch=2, grid=(seqs,),
+            in_specs=[
+                pl.BlockSpec((1, count, width_p, width_n), lambda s, *_: (s, 0, 0, 0)),
+                pl.BlockSpec((steps, count), lambda s, *_: (s, 0)),
+                pl.BlockSpec((slots, steps, width_n), lambda s, *_: (0, s, 0)),
+                pl.BlockSpec((steps, width_n), lambda s, *_: (s, 0)),
+                pl.BlockSpec((steps, width_n), lambda s, *_: (s, 0)),
+                pl.BlockSpec((steps, slots * width_p), lambda s, *_: (s, 0)),
+                pl.BlockSpec((steps, own * width_p), lambda s, *_: (s, 0)),
+                pl.BlockSpec((1, width_p, width_n), lambda s, *_: (s, 0, 0)),
+            ],
+            out_specs=[
+                pl.BlockSpec((1, count, width_p, width_n), lambda s, *_: (s, 0, 0, 0)),
+                pl.BlockSpec((steps, own * width_p), lambda s, *_: (s, 0)),
+            ],
+        ),
+        out_shape=[
+            jax.ShapeDtypeStruct(states.shape, f32),
+            jax.ShapeDtypeStruct((rows, own * width_p), f32),
+        ],
+        compiler_params=pltpu.CompilerParams(vmem_limit_bytes=VMEM),
+        cost_estimate=pl.CostEstimate(flops=20_000_000, bytes_accessed=32_000_000, transcendentals=0),
+        name="commit",
+    )(positions, accepted, states, factor, taken, in_vecs, out_vecs, token, draft, fold_in)
+    outputs = pl.pallas_call(
+        functools.partial(finish_kernel, plan),
+        grid=(1,),
+        in_specs=[whole((rows, own * width_p)), whole((rows, width_p))],
+        out_specs=whole((seqs, steps, own * width_p)),
+        out_shape=jax.ShapeDtypeStruct((seqs, steps, own * width_p), jnp.bfloat16),
+        name="finish",
+    )(own_out, received)
+    counted = summed_over(counted, "seq")
+    acceptance = counted[0, 0] / (lax.axis_size("seq") * seqs * steps)
+    return outputs, new_states, acceptance
+
+
+def dispatch(states, xbc, rates, level_weights, positions, accepted):
+    plan = Plan(lax.axis_size("level"), states, xbc, rates)
+    step = functools.partial(fast_on_device, plan) if plan.fits() else on_device
+    return step(states, xbc, rates, level_weights, positions, accepted)
+
+
 def solution(mesh):
     in_specs = (
         P("seq", "level", None, None),
@@ -161,5 +525,5 @@
     )
     out_specs = (P("seq", None, "level"), P("seq", "level", None, None), P())
     return jax.shard_map(
-        on_device, mesh=mesh, in_specs=in_specs, out_specs=out_specs, check_vma=False
-    )
+        dispatch, mesh=mesh, in_specs=in_specs, out_specs=out_specs, check_vma=False
+    )

time: 249 us -> 52.8 us (0.21)
  matrix products: 111 us -> 0 us
  blocking collectives: 82.5 us -> 0 us
  other arithmetic: 28.3 us -> 0.02 us
  Pallas kernels: 0 us -> 18.1 us
  starting transfers between devices: 1.63 us -> 13.8 us
  local copies, waits for them, and re-layouts: 22.1 us -> 10 us
  waiting for transfers between devices: 0.01 us -> 7.9 us
    dot_general x13 -> x0, matrix products: 111 us -> none  [the longest x1 38.7 us: on_device(): jnp.einsum('ab,sb,sbpn->sapn', same_head, leaving, states, precision=high...]
    all_gather x1 -> x0, blocking collectives: 75.7 us -> none  [on_device(): lax.all_gather(xbc, 'level', axis=2, tiled=True).astype(jnp.float32)]
    pallas_call x0 -> x4, Pallas kernels: none -> 18.1 us  [the longest x1 14 us: fast_on_device(): pl.pallas_call(functools.partial(states_kernel, plan), grid_spec=pltpu.Pr...]
    dot_general x1 -> x0, other arithmetic: 11.1 us -> none  [on_device(): jnp.einsum('ab,sb,sbpn->sapn', same_head, leaving, states, precision=high...]
    ppermute x0 -> x6, starting transfers between devices: none -> 9.33 us  [the longest x4 7.84 us: fast_on_device(): lax.ppermute(x, 'level', [(i, i ^ by) for i in range(devices)])]
    ppermute x0 -> x6, waiting for transfers between devices: none -> 7.9 us  [the longest x4 4.61 us: fast_on_device(): lax.ppermute(x, 'level', [(i, i ^ by) for i in range(devices)])]
    psum x1 -> x0, blocking collectives: 6.84 us -> none  [on_device(): total_taken = lax.psum(jnp.sum(accepted.astype(jnp.float32)), 'seq')]
    convert_element_type x9 -> x0, other arithmetic: 5.26 us -> none  [the longest x1 1.47 us: on_device(): outputs = summed.astype(jnp.bfloat16)]
  transfers between devices with their start and end apart: 2 -> 8, of which waited for: 0 -> 4; matrix products, arithmetic and copies ran while one was open for 25% -> 1% of each run, Pallas kernels for 0% -> 32%
where the time goes in v1:
time: 52.8 us; the launch traced here: 52.4 us
  Pallas kernels  18.1 us (34%)
  starting transfers between devices  13.8 us (26%)
  local copies, waits for them, and re-layouts  10 us (19%)
  waiting for transfers between devices  7.9 us (15%)
  between operations  2.49 us (5%)
    pallas_call x1, Pallas kernels, fast_on_device(): pl.pallas_call(functools.partial(states_kernel, plan), grid_spec=pltpu.Pr...  14 us
    unnamed x22, local copies, waits for them, and re-layouts  9.53 us
    ppermute x4, starting transfers between devices, fast_on_device(): lax.ppermute(x, 'level', [(i, i ^ by) for i in range(devices)])  7.84 us
    ppermute x4, waiting for transfers between devices, fast_on_device(): lax.ppermute(x, 'level', [(i, i ^ by) for i in range(devices)])  4.61 us
    ppermute x2, starting transfers between devices, passed_along(): lax.ppermute(x, axis, [(i, (i + by) % devices) for i in range(devices)])  4.49 us
    ppermute x2, waiting for transfers between devices, summed_over(): x = x + lax.ppermute(x, axis, [(i, i ^ by) for i in range(devices)])  3.29 us
    ppermute x2, starting transfers between devices, summed_over(): x = x + lax.ppermute(x, axis, [(i, i ^ by) for i in range(devices)])  1.49 us
    pallas_call x1, Pallas kernels, fast_on_device(): pl.pallas_call(functools.partial(assemble_kernel, plan), grid=(1,), in_sp...  1.48 us
  transfers between devices with their start and end apart: 8, of which 4 were waited for; matrix products, arithmetic and copies ran while one was open for 1% of the time, Pallas kernels for 32%

profile of v1, /device:TPU:0, one launch (start us, length us, event | category | flops | bytes accessed | tf_op | source)
XLA Modules:
  0.0 52.4 jit_solution(16892893129138238923)
XLA Ops:
  0.6 3.1 %collective-permute-start = (bf16[8,8,224]{2,1,0:T(8,128)(2,1)}, bf16[8,8,224]{2,1,0:T(8,128)(2,1)S(1)}, u32[]{:S(2)}, u32[]{:S(2)}) collective-permute-start(bf16[8,8,224]{2,1,0:T(8,128)(2,1)} %param.7), channel_id=1, source_target_pairs={{0,1},{1,0},{2,3},{3,2},{4,5},{5,4},{6,7},{7,6},{8,9},{9,8},{10,11... | collective-permute-start | bytes 86024 | tf_op jit(solution)/shard_map/ppermute | solution.py:428
  3.7 0.0 copy-start
  3.7 5.5 %copy-done = f32[8,60,64,128]{3,2,1,0:T(8,128)S(1)} copy-done((f32[8,60,64,128]{3,2,1,0:T(8,128)S(1)}, f32[8,60,64,128]{3,2,1,0:T(8,128)}, u32[]{:S(2)}) %copy-start) | copy-done | bytes 15728664
  9.2 0.0 copy-start.3
  9.2 0.8 %copy-done.3 = f32[8,8,24]{2,1,0:T(8,128)S(1)} copy-done((f32[8,8,24]{2,1,0:T(8,128)S(1)}, f32[8,8,24]{2,1,0:T(8,128)}, u32[]{:S(2)}) %copy-start.3) | copy-done | bytes 6168
  9.9 0.0 copy-start.4
  9.9 0.8 %copy-done.4 = f32[8,8,60]{2,1,0:T(8,128)S(1)} copy-done((f32[8,8,60]{2,1,0:T(8,128)S(1)}, f32[8,8,60]{2,1,0:T(8,128)}, u32[]{:S(2)}) %copy-start.4) | copy-done | bytes 15384
  10.7 0.0 copy-start.5
  10.7 0.7 %copy-done.5 = s32[8]{0:T(128)S(1)} copy-done((s32[8]{0:T(128)S(1)}, s32[8]{0:T(128)}, u32[]{:S(2)}) %copy-start.5) | copy-done | bytes 56
  11.3 0.0 copy-start.7
  11.3 0.7 %copy-done.7 = s32[8]{0:T(128)S(1)} copy-done((s32[8]{0:T(128)S(1)}, s32[8]{0:T(128)}, u32[]{:S(2)}) %copy-start.7) | copy-done | bytes 56
  12.0 0.0 copy-start.9
  12.0 0.0 copy-start.1
  12.0 0.0 copy-start.6
  12.0 0.0 copy-start.8
  12.0 1.2 %tables.1 = (f32[64,60]{1,0:T(8,128)S(1)}, f32[4,64,128]{2,1,0:T(8,128)S(1)}, f32[4,64,64]{2,1,0:T(8,128)S(1)}, f32[3,64,64]{2,1,0:T(8,128)S(1)}, bf16[8,64,128]{2,1,0:T(8,128)(2,1)S(1)}, /*index=5*/f32[8,128]{1,0:T(8,128)S(1)}) custom-call(s32[8]{0:T(128)S(1)} %copy-done.5, s32[8]{0:T(128)S(1)} %copy-done.7, f32[8,8,24]{2,1,0:T(8,128)S(1)} %copy-done.3, ...), custom_call_target="tpu_custom_call" | custom-call | flops 2000000 | bytes 3000000 | tf_op jit(solution)/shard_map/tables/pallas_call | solution.py:431
  13.2 0.1 collective-permute-start.4
  13.3 0.0 collective-permute-done
  13.3 0.0 copy-done.9
  13.3 4.1 %collective-permute-start.3 = (bf16[2,8,8,224]{3,2,1,0:T(8,128)(2,1)S(1)}, bf16[2,8,8,224]{3,2,1,0:T(8,128)(2,1)S(1)}, u32[]{:S(2)}, u32[]{:S(2)}) collective-permute-start(bf16[2,8,8,224]{3,2,1,0:T(8,128)(2,1)S(1)} %pad_maximum_fusion.pair_ref), channel_id=1, source_target_pairs={{0,6},{1,7},{2,4},{3,5},{4,2},{5,3},{6,0},{7,1},{8,14},{9,15},{10,... | collective-permute-start | bytes 172040 | tf_op jit(solution)/shard_map/ppermute | solution.py:428
  17.5 0.0 collective-permute-start.2
  17.5 0.6 %collective-permute-start.1 = (bf16[2,8,8,224]{3,2,1,0:T(8,128)(2,1)S(1)}, bf16[2,8,8,224]{3,2,1,0:T(8,128)(2,1)S(1)}, u32[]{:S(2)}, u32[]{:S(2)}) collective-permute-start(bf16[2,8,8,224]{3,2,1,0:T(8,128)(2,1)S(1)} %pad_maximum_fusion.pair_ref), channel_id=1, source_target_pairs={{0,2},{1,3},{2,0},{3,1},{4,6},{5,7},{6,4},{7,5},{8,10},{9,11},{10,... | collective-permute-start | bytes 172040 | tf_op jit(solution)/shard_map/ppermute | solution.py:428
  18.1 2.4 %collective-permute-done.3.refs_2_ = bf16[2,8,8,224]{3,2,1,0:T(8,128)(2,1)S(1)} collective-permute-done((bf16[2,8,8,224]{3,2,1,0:T(8,128)(2,1)S(1)}, bf16[2,8,8,224]{3,2,1,0:T(8,128)(2,1)S(1)}, u32[]{:S(2)}, u32[]{:S(2)}) %collective-permute-start.3) | collective-permute-done | bytes 57376 | tf_op jit(solution)/shard_map/ppermute | solution.py:428
  20.4 2.3 %collective-permute-done.2.refs_1_ = bf16[2,8,8,224]{3,2,1,0:T(8,128)(2,1)S(1)} collective-permute-done((bf16[2,8,8,224]{3,2,1,0:T(8,128)(2,1)S(1)}, bf16[2,8,8,224]{3,2,1,0:T(8,128)(2,1)S(1)}, u32[]{:S(2)}, u32[]{:S(2)}) %collective-permute-start.2) | collective-permute-done | bytes 57376 | tf_op jit(solution)/shard_map/ppermute | solution.py:428
  22.7 0.0 collective-permute-done.1.refs_0_
  22.7 0.0 copy-done.1
  22.7 1.5 %assemble.1 = (f32[64,128]{1,0:T(8,128)S(1)}, f32[64,128]{1,0:T(8,128)S(1)}, f32[64,256]{1,0:T(8,128)S(1)}, f32[64,192]{1,0:T(8,128)S(1)}, f32[64,64]{1,0:T(8,128)S(1)}) custom-call(bf16[2,8,8,224]{3,2,1,0:T(8,128)(2,1)S(1)} %pad_maximum_fusion.pair_ref, bf16[2,8,8,224]{3,2,1,0:T(8,128)(2,1)S(1)} %collective-permute-done.1.refs_0_, ...), custom_call_target="tpu_custom_call" | custom-call | flops 2000000 | bytes 3000000 | tf_op jit(solution)/shard_map/assemble/pallas_call | solution.py:454
  24.2 4.4 %collective-permute-start.5 = (f32[64,64]{1,0:T(8,128)S(1)}, f32[64,64]{1,0:T(8,128)S(1)}, u32[]{:S(2)}, u32[]{:S(2)}) collective-permute-start(f32[64,64]{1,0:T(8,128)S(1)} %get-tuple-element.26), channel_id=1, source_target_pairs={{0,1},{1,2},{2,3},{3,4},{4,5},{5,6},{6,7},{7,0},{8,9},{9,10},{10,1... | collective-permute-start | bytes 49160 | tf_op jit(solution)/shard_map/ppermute | solution.py:20
  28.6 0.0 collective-permute-start.6
  28.6 1.2 %collective-permute-done.6 = f32[8,128]{1,0:T(8,128)S(1)} collective-permute-done((f32[8,128]{1,0:T(8,128)S(1)}, f32[8,128]{1,0:T(8,128)S(1)}, u32[]{:S(2)}, u32[]{:S(2)}) %collective-permute-start.6) | collective-permute-done | bytes 4128 | tf_op jit(solution)/shard_map/ppermute | solution.py:413
  29.8 1.5 %collective-permute-start.7 = (f32[8,128]{1,0:T(8,128)S(1)}, f32[8,128]{1,0:T(8,128)S(1)}, u32[]{:S(2)}, u32[]{:S(2)}) collective-permute-start(f32[8,128]{1,0:T(8,128)S(1)} %add.6), channel_id=1, source_target_pairs={{0,16},{8,24},{16,0},{24,8},{1,17},{9,25},{17,1},{25,9},{2,18},{10... | collective-permute-start | bytes 12296 | tf_op jit(solution)/shard_map/ppermute | solution.py:413
  31.3 2.1 %collective-permute-done.7 = f32[8,128]{1,0:T(8,128)S(1)} collective-permute-done((f32[8,128]{1,0:T(8,128)S(1)}, f32[8,128]{1,0:T(8,128)S(1)}, u32[]{:S(2)}, u32[]{:S(2)}) %collective-permute-start.7) | collective-permute-done | bytes 4128 | tf_op jit(solution)/shard_map/ppermute | solution.py:413
  33.4 0.5 slice.3
  34.6 0.0 collective-permute-done.4.fold_ref
  34.6 0.0 copy-done.6
  34.6 0.0 copy-done.8
  34.6 14.0 %commit.1 = (f32[8,60,64,128]{3,2,1,0:T(8,128)}, f32[64,192]{1,0:T(8,128)S(1)}) custom-call(s32[8]{0:T(128)S(1)} %copy-done.6, s32[8]{0:T(128)S(1)} %copy-done.8, f32[8,60,64,128]{3,2,1,0:T(8,128)S(1)} %copy-done.1, f32[64,60]{1,0:T(8,128)S(1)} %get-tuple-element.16.refs_4_.factor_ref, f32[4,64,128]{2,1,0:T(8,128)S(1)} %get-tuple-element.17.taken_ref, ...), custom_call_target="tpu_custom_call" | custom-call | flops 20000000 | bytes 32000000 | tf_op jit(solution)/shard_map/commit/pallas_call | solution.py:471
  48.6 0.0 copy-start.2
  48.6 0.6 %copy-done.2 = f32[64,192]{1,0:T(8,128)} copy-done((f32[64,192]{1,0:T(8,128)}, f32[64,192]{1,0:T(8,128)S(1)}, u32[]{:S(2)}) %copy-start.2) | copy-done | bytes 49176
  49.2 0.0 collective-permute-done.5.received_ref
  49.2 0.0 copy-start.10
  49.2 0.6 %copy-done.10 = f32[64,64]{1,0:T(8,128)} copy-done((f32[64,64]{1,0:T(8,128)}, f32[64,64]{1,0:T(8,128)S(1)}, u32[]{:S(2)}) %copy-start.10) | copy-done | bytes 16408
  49.8 1.5 %finish.1 = bf16[8,8,192]{2,1,0:T(8,128)(2,1)} custom-call(f32[64,192]{1,0:T(8,128)} %copy-done.2, f32[64,64]{1,0:T(8,128)} %copy-done.10), custom_call_target="tpu_custom_call" | custom-call | tf_op jit(solution)/shard_map/finish/pallas_call | solution.py:498
  (3 shorter events, 0.0 us)
Async XLA Ops:
  0.6 12.6 %collective-permute-start = (bf16[8,8,224]{2,1,0:T(8,128)(2,1)}, bf16[8,8,224]{2,1,0:T(8,128)(2,1)S(1)}, u32[]{:S(2)}, u32[]{:S(2)}) collective-permute-start(bf16[8,8,224]{2,1,0:T(8,128)(2,1)} %param.7), channel_id=1, source_target_pairs={{0,1},{1,0},{2,3},{3,2},{4,5},{5,4},{6,7},{7,6},{8,9},{9,8},{10,11... | collective-permute-start | bytes 86024 | tf_op jit(solution)/shard_map/ppermute | solution.py:428
  3.7 5.5 %copy-start = (f32[8,60,64,128]{3,2,1,0:T(8,128)S(1)}, f32[8,60,64,128]{3,2,1,0:T(8,128)}, u32[]{:S(2)}) copy-start(f32[8,60,64,128]{3,2,1,0:T(8,128)} %states_ref.3) | copy-start | bytes 47185924
  9.2 0.8 %copy-start.3 = (f32[8,8,24]{2,1,0:T(8,128)S(1)}, f32[8,8,24]{2,1,0:T(8,128)}, u32[]{:S(2)}) copy-start(f32[8,8,24]{2,1,0:T(8,128)} %rates_ref.1) | copy-start | bytes 18436
  9.9 0.8 %copy-start.4 = (f32[8,8,60]{2,1,0:T(8,128)S(1)}, f32[8,8,60]{2,1,0:T(8,128)}, u32[]{:S(2)}) copy-start(f32[8,8,60]{2,1,0:T(8,128)} %weights_ref.1) | copy-start | bytes 46084
  10.7 0.7 %copy-start.5 = (s32[8]{0:T(128)S(1)}, s32[8]{0:T(128)}, u32[]{:S(2)}) copy-start(s32[8]{0:T(128)} %pos.3) | copy-start | bytes 100
  11.3 0.7 %copy-start.7 = (s32[8]{0:T(128)S(1)}, s32[8]{0:T(128)}, u32[]{:S(2)}) copy-start(s32[8]{0:T(128)} %acc.3) | copy-start | bytes 100
  12.0 1.3 %copy-start.9 = (bf16[8,8,224]{2,1,0:T(8,128)(2,1)S(1)}, bf16[8,8,224]{2,1,0:T(8,128)(2,1)}, u32[]{:S(2)}) copy-start(bf16[8,8,224]{2,1,0:T(8,128)(2,1)} %param.7) | copy-start | bytes 86020
  12.0 10.7 %copy-start.1 = (f32[8,60,64,128]{3,2,1,0:T(8,128)S(1)}, f32[8,60,64,128]{3,2,1,0:T(8,128)}, u32[]{:S(2)}) copy-start(f32[8,60,64,128]{3,2,1,0:T(8,128)} %states_ref.3) | copy-start | bytes 47185924
  12.0 22.6 %copy-start.6 = (s32[8]{0:T(128)S(1)}, s32[8]{0:T(128)}, u32[]{:S(2)}) copy-start(s32[8]{0:T(128)} %pos.3) | copy-start | bytes 100
  12.0 22.6 %copy-start.8 = (s32[8]{0:T(128)S(1)}, s32[8]{0:T(128)}, u32[]{:S(2)}) copy-start(s32[8]{0:T(128)} %acc.3) | copy-start | bytes 100
  13.2 21.4 %collective-permute-start.4 = (bf16[8,64,128]{2,1,0:T(8,128)(2,1)S(1)}, bf16[8,64,128]{2,1,0:T(8,128)(2,1)S(1)}, u32[]{:S(2)}, u32[]{:S(2)}) collective-permute-start(bf16[8,64,128]{2,1,0:T(8,128)(2,1)S(1)} %get-tuple-element.24), channel_id=1, source_target_pairs={{0,1},{1,2},{2,3},{3,4},{4,5},{5,6},{6,7},{7,0},{8,9},{9,10},{10,1... | collective-permute-start | bytes 393224 | tf_op jit(solution)/shard_map/ppermute | solution.py:20
  13.3 7.1 %collective-permute-start.3 = (bf16[2,8,8,224]{3,2,1,0:T(8,128)(2,1)S(1)}, bf16[2,8,8,224]{3,2,1,0:T(8,128)(2,1)S(1)}, u32[]{:S(2)}, u32[]{:S(2)}) collective-permute-start(bf16[2,8,8,224]{3,2,1,0:T(8,128)(2,1)S(1)} %pad_maximum_fusion.pair_ref), channel_id=1, source_target_pairs={{0,6},{1,7},{2,4},{3,5},{4,2},{5,3},{6,0},{7,1},{8,14},{9,15},{10,... | collective-permute-start | bytes 172040 | tf_op jit(solution)/shard_map/ppermute | solution.py:428
  17.5 5.2 %collective-permute-start.2 = (bf16[2,8,8,224]{3,2,1,0:T(8,128)(2,1)S(1)}, bf16[2,8,8,224]{3,2,1,0:T(8,128)(2,1)S(1)}, u32[]{:S(2)}, u32[]{:S(2)}) collective-permute-start(bf16[2,8,8,224]{3,2,1,0:T(8,128)(2,1)S(1)} %pad_maximum_fusion.pair_ref), channel_id=1, source_target_pairs={{0,4},{1,5},{2,6},{3,7},{4,0},{5,1},{6,2},{7,3},{8,12},{9,13},{10,... | collective-permute-start | bytes 172040 | tf_op jit(solution)/shard_map/ppermute | solution.py:428
  17.5 5.2 %collective-permute-start.1 = (bf16[2,8,8,224]{3,2,1,0:T(8,128)(2,1)S(1)}, bf16[2,8,8,224]{3,2,1,0:T(8,128)(2,1)S(1)}, u32[]{:S(2)}, u32[]{:S(2)}) collective-permute-start(bf16[2,8,8,224]{3,2,1,0:T(8,128)(2,1)S(1)} %pad_maximum_fusion.pair_ref), channel_id=1, source_target_pairs={{0,2},{1,3},{2,0},{3,1},{4,6},{5,7},{6,4},{7,5},{8,10},{9,11},{10,... | collective-permute-start | bytes 172040 | tf_op jit(solution)/shard_map/ppermute | solution.py:428
  24.2 25.0 %collective-permute-start.5 = (f32[64,64]{1,0:T(8,128)S(1)}, f32[64,64]{1,0:T(8,128)S(1)}, u32[]{:S(2)}, u32[]{:S(2)}) collective-permute-start(f32[64,64]{1,0:T(8,128)S(1)} %get-tuple-element.26), channel_id=1, source_target_pairs={{0,1},{1,2},{2,3},{3,4},{4,5},{5,6},{6,7},{7,0},{8,9},{9,10},{10,1... | collective-permute-start | bytes 49160 | tf_op jit(solution)/shard_map/ppermute | solution.py:20
  28.6 1.2 %collective-permute-start.6 = (f32[8,128]{1,0:T(8,128)S(1)}, f32[8,128]{1,0:T(8,128)S(1)}, u32[]{:S(2)}, u32[]{:S(2)}) collective-permute-start(f32[8,128]{1,0:T(8,128)S(1)} %get-tuple-element.28), channel_id=1, source_target_pairs={{0,8},{8,0},{16,24},{24,16},{1,9},{9,1},{17,25},{25,17},{2,10},{10... | collective-permute-start | bytes 12296 | tf_op jit(solution)/shard_map/ppermute | solution.py:413
  29.8 3.6 %collective-permute-start.7 = (f32[8,128]{1,0:T(8,128)S(1)}, f32[8,128]{1,0:T(8,128)S(1)}, u32[]{:S(2)}, u32[]{:S(2)}) collective-permute-start(f32[8,128]{1,0:T(8,128)S(1)} %add.6), channel_id=1, source_target_pairs={{0,16},{8,24},{16,0},{24,8},{1,17},{9,25},{17,1},{25,9},{2,18},{10... | collective-permute-start | bytes 12296 | tf_op jit(solution)/shard_map/ppermute | solution.py:413
  48.6 0.6 %copy-start.2 = (f32[64,192]{1,0:T(8,128)}, f32[64,192]{1,0:T(8,128)S(1)}, u32[]{:S(2)}) copy-start(f32[64,192]{1,0:T(8,128)S(1)} %get-tuple-element.25.own_ref) | copy-start | bytes 147460
  49.2 0.6 %copy-start.10 = (f32[64,64]{1,0:T(8,128)}, f32[64,64]{1,0:T(8,128)S(1)}, u32[]{:S(2)}) copy-start(f32[64,64]{1,0:T(8,128)S(1)} %collective-permute-done.5.received_ref) | copy-start | bytes 49156

commit v2 on v1

--- a/solution.py
+++ b/solution.py
@@ -12,7 +12,9 @@
 N = 128
 L = 20
 K = 8
+PARTS = 2
 VMEM = 24 * 2**20
+BASE_VMEM = 40 * 2**20
 
 
 def passed_along(x, axis, by):
@@ -171,10 +173,13 @@
     )
 
 
-def weighted_queries(factor, out_vecs):
-    high, low = split(factor * out_vecs)
-    rows = jnp.concatenate([high, low], axis=0)
-    return jnp.concatenate([rows, rows], axis=1)
+def applied(sums, queries):
+    lane = lax.broadcasted_iota(jnp.int32, (sums.shape[1], queries.shape[0]), 1)
+    total = None
+    for t in range(queries.shape[0]):
+        term = jnp.sum(sums[t] * queries[t : t + 1, :], axis=1, keepdims=True)
+        total = jnp.broadcast_to(term, lane.shape) if t == 0 else jnp.where(lane == t, term, total)
+    return total.T
 
 
 class Plan:
@@ -192,7 +197,7 @@
         self.starts = [0] + [L - self.offset + i * L for i in range(self.own)] + [self.count]
         self.value_width = self.heads * self.width_p
 
-    def fits(self):
+    def fits(self, groups):
         return (
             self.count % L == 0
             and L - self.offset == self.offset
@@ -200,6 +205,8 @@
             and self.devices > 1
             and self.heads == self.own * self.devices
             and self.steps == 8
+            and groups >= 4
+            and groups & (groups - 1) == 0
             and self.low <= self.offset
         )
 
@@ -208,20 +215,26 @@
         return [(j, first + j - self.starts[slot]) for j in range(self.starts[slot], self.starts[slot + 1])]
 
 
-def tables_kernel(plan, pos, acc, rates_ref, weights_ref, states_ref, factor_ref, taken_ref,
-                  decay_ref, mix_ref, fold_ref, count_ref):
+def tables_kernel(plan, pos_hbm, acc_hbm, rates_hbm, weights_hbm, states_hbm, factor_ref, taken_ref,
+                  decay_ref, mix_ref, fold_ref, count_ref, pos, acc, rates_ref, weights_ref, states_ref, sems, state_sems):
+    copies = [
+        pltpu.make_async_copy(source, target, sems.at[n])
+        for n, (source, target) in enumerate(
+            [(pos_hbm, pos), (acc_hbm, acc), (rates_hbm, rates_ref), (weights_hbm, weights_ref)]
+        )
+    ]
+    state_copies = [
+        pltpu.make_async_copy(
+            states_hbm.at[s, pl.ds(plan.count - plan.offset, plan.offset)], states_ref.at[s], state_sems.at[s]
+        )
+        for s in range(plan.seqs)
+    ]
+    for copy in copies + state_copies:
+        copy.start()
+    for copy in copies:
+        copy.wait()
     rows, steps, seqs = plan.rows, plan.steps, plan.seqs
     first_head = lax.axis_index("level") * plan.own
-    for s in range(seqs):
-        p, q = pos[s], pos[s] + acc[s]
-        top = highest_bit(jnp.bitwise_xor(p, q))
-        leaving = jnp.where(top >= plan.offset, p, 0)
-        total = None
-        for k in range(plan.offset):
-            bit = (jnp.right_shift(leaving, k) & 1) * (k < top).astype(jnp.int32)
-            term = states_ref[s, k] * bit.astype(jnp.float32)
-            total = term if total is None else total + term
-        fold_ref[s] = total.astype(fold_ref.dtype)
     count_ref[...] = jnp.full(count_ref.shape, sum(acc[s] for s in range(seqs)).astype(jnp.float32))
     rate = rates_ref[...].reshape(rows, plan.heads)
     weight = weights_ref[...].reshape(rows, plan.count)
@@ -263,11 +276,23 @@
             mix_ref[i - 1] = mix * weight[:, first : first + 1]
     occupied = jnp.right_shift(place1, (lane + plan.offset) % L) & 1
     factor_ref[...] = weight * occupied.astype(jnp.float32) * scale
+    for s in range(seqs):
+        p, q = pos[s], pos[s] + acc[s]
+        top = highest_bit(jnp.bitwise_xor(p, q))
+        leaving = jnp.where(top >= plan.offset, p, 0)
+        state_copies[s].wait()
+        total = None
+        for k in range(plan.offset):
+            bit = (jnp.right_shift(leaving, k) & 1) * (k < top).astype(jnp.int32)
+            term = states_ref[s, k] * bit.astype(jnp.float32)
+            total = term if total is None else total + term
+        fold_ref[s] = total.astype(fold_ref.dtype)
 
 
 def assemble_kernel(plan, pair_ref, *refs):
-    *far_refs, states_ref, factor_ref, decay_ref, mix_ref = refs[: plan.devices // 2 - 1 + 4]
-    in_ref, out_ref, token_ref, draft_ref, send_ref, all_ref = refs[plan.devices // 2 - 1 + 4 :]
+    *far_refs, sums_ref, decay_ref, mix_ref, count_ref, counted_ref = refs[: plan.devices // 2 - 1 + 5]
+    in_ref, out_ref, token_ref, draft_ref, send_ref, sum_ref, all_ref = refs[plan.devices // 2 - 1 + 5 :]
+    sum_ref[...] = count_ref[...] + counted_ref[...]
     rows, shard = plan.rows, plan.shard
     me = lax.axis_index("level")
     for half, ref in enumerate([pair_ref, *far_refs]):
@@ -315,104 +340,152 @@
     steps = plan.steps
     for s in range(plan.seqs):
         at = slice(s * steps, (s + 1) * steps)
-        query = out_vecs[at]
-        total = None
-        for k, (j, _) in enumerate(plan.levels(plan.own)):
-            left = weighted_queries(factor_ref[at, j : j + 1], query)
-            right = jnp.concatenate(split(states_ref[s, k]), axis=1)
-            term = dot_nt(left, right)
-            total = term if total is None else total + term
-        send_ref[at] = total[:steps] + total[steps:] + drafts[-1][at]
-
-
-def states_kernel(plan, pos, acc, states_ref, factor_ref, taken_ref, in_ref, out_ref, token_ref,
-                  draft_ref, fold_ref, new_ref, own_ref):
+        send_ref[at] = applied(sums_ref[s, plan.own], out_vecs[at]) + drafts[-1][at]
+
+
+def base_kernel(plan, pos, acc, *refs):
+    parts = plan.count // plan.offset
+    states_refs = refs[:parts]
+    factor_ref, taken_ref, new_hbm, sums_ref, low_ref, merged_ref, new_ref, wide_ref, sems = refs[parts:]
     s = pl.program_id(0)
     steps, width_p, width_n = plan.steps, plan.width_p, plan.width_n
     p = pos[s]
-    a = acc[s]
-    q = p + a
+    q = p + acc[s]
     top = highest_bit(jnp.bitwise_xor(p, q))
     bound = jnp.maximum(top, 0)
-    below = jnp.left_shift(1, bound) - 1
     upto = jnp.where(top < 0, 0, jnp.left_shift(2, bound) - 1)
     staying = p & q & jnp.bitwise_not(upto)
-    leaving = jnp.where(top < 0, 0, p & below)
+    leaving = jnp.where(top < 0, 0, p & (jnp.left_shift(1, bound) - 1))
+    side = lax.rem(s, 2)
+
+    def sent(i, s, side):
+        at = pl.ds(plan.starts[i], plan.starts[i + 1] - plan.starts[i])
+        return pltpu.make_async_copy(new_ref.at[side, at], new_hbm.at[s, at], sems.at[side, i])
+
+    for j in range(plan.count):
+        wide_ref[j] = jnp.broadcast_to(factor_ref[:, j : j + 1], (steps, width_n))
+    half = width_p // PARTS
+    for i in range(plan.slots):
+
+        @pl.when(s >= 2)
+        def _():
+            sent(i, s - 2, side).wait()
+
+        grown = taken_ref[i, 0:1, :]
+        for part in range(PARTS):
+            at = slice(part * half, (part + 1) * half)
+            sums = [None] * steps
+            merged = None
+            for j, level in plan.levels(i):
+                state = states_refs[j // plan.offset][0, j % plan.offset, at, :]
+                kept = (jnp.right_shift(staying, level) & 1).astype(jnp.float32)
+                new = state * (grown * kept)
+                new_ref[side, j, at, :] = new
+                if level < plan.low:
+                    low_ref[0, i - 1, level, at, :] = new
+                left = (jnp.right_shift(leaving, level) & 1).astype(jnp.float32)
+                term = state * left
+                merged = term if merged is None else merged + term
+                for t in range(steps):
+                    term = state * wide_ref[j, t : t + 1, :]
+                    sums[t] = term if sums[t] is None else sums[t] + term
+            merged_ref[0, i, at, :] = merged
+            for t in range(steps):
+                sums_ref[0, i, t, at, :] = sums[t]
+        sent(i, s, side).start()
+
+    @pl.when(s == plan.seqs - 1)
+    def _():
+        for i in range(plan.slots):
+            if plan.seqs > 1:
+                sent(i, s - 1, 1 - side).wait()
+            sent(i, s, side).wait()
+
+
+def settle_kernel(plan, pos, acc, sums_ref, low_ref, merged_ref, taken_ref, in_ref, out_ref, token_ref,
+                  draft_ref, fold_ref, old_hbm, new_hbm, own_ref, low_buf, top_buf, low_sems, top_sems):
+    del old_hbm
+    steps, width_p, width_n, low = plan.steps, plan.width_p, plan.width_n, plan.low
     step = lax.broadcasted_iota(jnp.int32, (2 * steps, width_n), 0) % steps
-    in_vecs = in_ref[...]
-    in_twice = jnp.concatenate([in_vecs, in_vecs], axis=0)
-    groups = []
-    for g in range(plan.low + 1):
-        level = bound if g == plan.low else g
-        wanted = (jnp.right_shift(q, level) & 1) == 1
-        if g < plan.low:
-            wanted = wanted & (top != g)
-        start = jnp.left_shift(jnp.right_shift(q, level + 1), level + 1)
-        last = jnp.minimum(start + jnp.left_shift(1, level) - p, a)
-        last = jnp.where(wanted, last, 0)
-        inside = (step >= start - p) & (step < last)
-        groups.append(jnp.where(inside, in_twice, 0.0).astype(jnp.bfloat16))
-    spread = jnp.concatenate(split(token_ref[...]), axis=0)
-    added = lax.dot_general(
-        spread, jnp.concatenate(groups, axis=1), (((0,), (0,)), ((), ())),
-        preferred_element_type=jnp.float32,
-    )
-
-    def tokens(i, g):
-        return added[i * width_p : (i + 1) * width_p, g * width_n : (g + 1) * width_n]
-
-    query = out_ref[...]
-    for i in range(plan.slots):
-        grown = taken_ref[i, 0:1, :]
-        merged = None
-        total = None
-        for j, level in plan.levels(i):
-            state = states_ref[0, j]
-            kept = (jnp.right_shift(staying, level) & 1).astype(jnp.float32)
-            new = state * (grown * kept)
-            if level < plan.low:
-                new = new + tokens(i, level)
-            new_ref[0, j] = new
-            left = (jnp.right_shift(leaving, level) & 1).astype(jnp.float32)
-            term = state * left
-            merged = term if merged is None else merged + term
-            if i < plan.own:
-                rows = weighted_queries(factor_ref[:, j : j + 1], query)
-                term = dot_nt(rows, jnp.concatenate(split(state), axis=1))
-                total = term if total is None else total + term
-        if i < plan.own:
+    copies = []
+    for s in range(plan.seqs):
+        rows = slice(s * steps, (s + 1) * steps)
+        p = pos[s]
+        a = acc[s]
+        q = p + a
+        top = highest_bit(jnp.bitwise_xor(p, q))
+        bound = jnp.maximum(top, 0)
+        in_vecs = in_ref[rows]
+        in_twice = jnp.concatenate([in_vecs, in_vecs], axis=0)
+        groups = []
+        for g in range(low + 1):
+            level = bound if g == low else g
+            wanted = (jnp.right_shift(q, level) & 1) == 1
+            if g < low:
+                wanted = wanted & (top != g)
+            start = jnp.left_shift(jnp.right_shift(q, level + 1), level + 1)
+            last = jnp.minimum(start + jnp.left_shift(1, level) - p, a)
+            last = jnp.where(wanted, last, 0)
+            inside = (step >= start - p) & (step < last)
+            groups.append(jnp.where(inside, in_twice, 0.0).astype(jnp.bfloat16))
+        spread = jnp.concatenate(split(token_ref[rows]), axis=0)
+        added = lax.dot_general(
+            spread, jnp.concatenate(groups, axis=1), (((0,), (0,)), ((), ())),
+            preferred_element_type=jnp.float32,
+        )
+
+        def tokens(i, g):
+            return added[i * width_p : (i + 1) * width_p, g * width_n : (g + 1) * width_n]
+
+        for i in range(plan.slots):
+            grown = taken_ref[i, s * steps : s * steps + 1, :]
+            merged = merged_ref[s, i]
+            here = top >= 0
+            if i == 0:
+                here = top >= plan.offset
+                merged = merged + fold_ref[s].astype(jnp.float32)
+            if i == plan.own:
+                here = here & (top < plan.offset)
+            value = merged * grown + tokens(i, low)
+            top_buf[s, i] = value
+            base = plan.starts[i] - (plan.offset if i == 0 else 0)
+            far = here & (top >= low)
+            copy = pltpu.make_async_copy(
+                top_buf.at[s, i], new_hbm.at[s, base + jnp.where(far, top, low)], top_sems.at[s, i]
+            )
+            copies.append((far, copy))
+            pl.when(far)(copy.start)
+            if i > 0:
+                for g in range(low):
+                    low_buf[s, i - 1, g] = low_ref[s, i - 1, g] + tokens(i, g)
+
+                @pl.when(here & (top < low))
+                def _():
+                    low_buf[s, i - 1, bound] = value
+
+                copy = pltpu.make_async_copy(
+                    low_buf.at[s, i - 1], new_hbm.at[s, pl.ds(plan.starts[i], low)], low_sems.at[s, i - 1]
+                )
+                copies.append((None, copy))
+                copy.start()
+        query = out_ref[rows]
+        for i in range(plan.own):
             at = slice(i * width_p, (i + 1) * width_p)
-            own_ref[:, at] = total[:steps] + total[steps:] + draft_ref[:, at]
-        base = plan.starts[i] - (plan.offset if i == 0 else 0)
-        here = top >= 0
-        if i == 0:
-            here = top >= plan.offset
-            merged = merged + fold_ref[0].astype(jnp.float32)
-        if i == plan.own:
-            here = here & (top < plan.offset)
-
-        @pl.when(here)
-        def _():
-            new_ref[0, base + top] = merged * grown + tokens(i, plan.low)
-
-
-def finish_kernel(plan, own_ref, received_ref, out_ref):
+            own_ref[rows, at] = applied(sums_ref[s, i], query) + draft_ref[rows, at]
+    for far, copy in copies:
+        if far is None:
+            copy.wait()
+        else:
+            pl.when(far)(copy.wait)
+
+
+def finish_kernel(plan, scale, own_ref, received_ref, count_ref, counted_ref, out_ref, share_ref):
     width_p = plan.width_p
     own = own_ref[...]
     first = own[:, :width_p] + received_ref[...]
     total = jnp.concatenate([first, own[:, width_p:]], axis=1)
     out_ref[...] = total.reshape(out_ref.shape).astype(out_ref.dtype)
-
-
-def summed_over(x, axis):
-    devices = lax.axis_size(axis)
-    if devices & (devices - 1):
-        return lax.psum(x, axis)
-    by = 1
-    while by < devices:
-        x = x + lax.ppermute(x, axis, [(i, i ^ by) for i in range(devices)])
-        by *= 2
-    return x
+    share_ref[...] = ((count_ref[...] + counted_ref[...]) * scale)[:1, :1]
 
 
 def whole(shape, index=None):
@@ -425,17 +498,24 @@
     count, slots, own = plan.count, plan.slots, plan.own
     width_p, width_n = plan.width_p, plan.width_n
     f32 = jnp.float32
+    groups = lax.axis_size("seq")
     swap = lambda x, by: lax.ppermute(x, "level", [(i, i ^ by) for i in range(devices)])
-    boundary = ((seqs, plan.offset, width_p, width_n), (0, count // plan.offset - 1, 0, 0))
-    beside = swap(xbc, 1)
+    parts = count // plan.offset
+    hbm = pl.BlockSpec(memory_space=pltpu.HBM)
+    pair = jnp.stack([xbc, swap(xbc, 1)])
+    far = [swap(pair, by) for by in range(2, devices, 2)]
     factor, taken, decay, mix, fold, counted = pl.pallas_call(
         functools.partial(tables_kernel, plan),
-        grid_spec=pltpu.PrefetchScalarGridSpec(
-            num_scalar_prefetch=2, grid=(1,),
-            in_specs=[whole(rates.shape), whole(level_weights.shape), whole(*boundary)],
-            out_specs=[whole((rows, count)), whole((slots, rows, width_n)), whole((slots, rows, width_p)),
-                       whole((own, rows, rows)), whole((seqs, width_p, width_n)), whole((8, 128))],
-        ),
+        grid=(1,),
+        in_specs=[pl.BlockSpec(memory_space=pltpu.HBM)] * 5,
+        out_specs=[whole((rows, count)), whole((slots, rows, width_n)), whole((slots, rows, width_p)),
+                   whole((own, rows, rows)), whole((seqs, width_p, width_n)), whole((8, 128))],
+        scratch_shapes=[
+            pltpu.SMEM((seqs,), jnp.int32), pltpu.SMEM((seqs,), jnp.int32),
+            pltpu.VMEM(rates.shape, f32), pltpu.VMEM(level_weights.shape, f32),
+            pltpu.VMEM((seqs, plan.offset, width_p, width_n), f32),
+            pltpu.SemaphoreType.DMA((4,)), pltpu.SemaphoreType.DMA((seqs,)),
+        ],
         out_shape=[
             jax.ShapeDtypeStruct((rows, count), f32),
             jax.ShapeDtypeStruct((slots, rows, width_n), f32),
@@ -444,73 +524,108 @@
             jax.ShapeDtypeStruct((seqs, width_p, width_n), jnp.bfloat16),
             jax.ShapeDtypeStruct((8, 128), f32),
         ],
-        compiler_params=pltpu.CompilerParams(vmem_limit_bytes=VMEM),
+        compiler_params=pltpu.CompilerParams(vmem_limit_bytes=40 * 2**20),
         cost_estimate=pl.CostEstimate(flops=2_000_000, bytes_accessed=3_000_000, transcendentals=0),
         name="tables",
-    )(positions, accepted, rates, level_weights, states)
-    pair = jnp.stack([xbc, beside])
-    far = [swap(pair, by) for by in range(2, devices, 2)]
+    )(*[pltpu.with_memory_space_constraint(x, pltpu.HBM) for x in (positions, accepted, rates, level_weights, states)])
     fold_in = passed_along(fold, "level", 1)
-    in_vecs, out_vecs, token, draft, send = pl.pallas_call(
+    base_states, sums, low, merged = pl.pallas_call(
+        functools.partial(base_kernel, plan),
+        grid_spec=pltpu.PrefetchScalarGridSpec(
+            num_scalar_prefetch=2, grid=(seqs,),
+            in_specs=[
+                pl.BlockSpec((1, plan.offset, width_p, width_n), lambda s, *_, part=part: (s, part, 0, 0))
+                for part in range(parts)
+            ] + [
+                pl.BlockSpec((steps, count), lambda s, *_: (s, 0)),
+                pl.BlockSpec((slots, steps, width_n), lambda s, *_: (0, s, 0)),
+            ],
+            out_specs=[
+                hbm,
+                pl.BlockSpec((1, slots, steps, width_p, width_n), lambda s, *_: (s, 0, 0, 0, 0)),
+                pl.BlockSpec((1, own, plan.low, width_p, width_n), lambda s, *_: (s, 0, 0, 0, 0)),
+                pl.BlockSpec((1, slots, width_p, width_n), lambda s, *_: (s, 0, 0, 0)),
+            ],
+            scratch_shapes=[
+                pltpu.VMEM((2, count, width_p, width_n), f32),
+                pltpu.VMEM((count, steps, width_n), f32),
+                pltpu.SemaphoreType.DMA((2, slots)),
+            ],
+        ),
+        out_shape=[
+            jax.ShapeDtypeStruct(states.shape, f32),
+            jax.ShapeDtypeStruct((seqs, slots, steps, width_p, width_n), f32),
+            jax.ShapeDtypeStruct((seqs, own, plan.low, width_p, width_n), f32),
+            jax.ShapeDtypeStruct((seqs, slots, width_p, width_n), f32),
+        ],
+        compiler_params=pltpu.CompilerParams(vmem_limit_bytes=BASE_VMEM),
+        cost_estimate=pl.CostEstimate(flops=20_000_000, bytes_accessed=32_000_000, transcendentals=0),
+        name="base",
+    )(positions, accepted, *[states] * parts, factor, taken)
+    meet = lambda x, by: lax.ppermute(x, "seq", [(i, i ^ by) for i in range(groups)])
+    counted_in = meet(counted, 1)
+    in_vecs, out_vecs, token, draft, send, summed = pl.pallas_call(
         functools.partial(assemble_kernel, plan),
         grid=(1,),
         in_specs=[whole(pair.shape)] * (1 + len(far)) + [
-            whole(*boundary), whole(factor.shape), whole(decay.shape), whole(mix.shape)],
+            whole(sums.shape), whole(decay.shape), whole(mix.shape),
+            whole(counted.shape), whole(counted.shape)],
         out_specs=[whole((rows, width_n))] * 2 + [whole((rows, slots * width_p)), whole((rows, own * width_p)),
-                                                  whole((rows, width_p))],
+                                                  whole((rows, width_p)), whole(counted.shape)],
         out_shape=[jax.ShapeDtypeStruct((rows, width_n), f32)] * 2 + [
             jax.ShapeDtypeStruct((rows, slots * width_p), f32),
             jax.ShapeDtypeStruct((rows, own * width_p), f32),
-            jax.ShapeDtypeStruct((rows, width_p), f32)],
+            jax.ShapeDtypeStruct((rows, width_p), f32),
+            jax.ShapeDtypeStruct(counted.shape, f32)],
         scratch_shapes=[pltpu.VMEM((devices, rows, plan.shard), jnp.bfloat16)],
         compiler_params=pltpu.CompilerParams(vmem_limit_bytes=VMEM),
         cost_estimate=pl.CostEstimate(flops=2_000_000, bytes_accessed=3_000_000, transcendentals=0),
         name="assemble",
-    )(pair, *far, states, factor, decay, mix)
+    )(pair, *far, sums, decay, mix, counted, counted_in)
+    by = 2
+    while 2 * by < groups:
+        summed = summed + meet(summed, by)
+        by *= 2
+    summed_in = meet(summed, by)
     received = passed_along(send, "level", 1)
+    settled = [whole(sums.shape), whole(low.shape), whole(merged.shape), whole(taken.shape),
+               whole(in_vecs.shape), whole(out_vecs.shape), whole(token.shape), whole(draft.shape), whole(fold.shape)]
     new_states, own_out = pl.pallas_call(
-        functools.partial(states_kernel, plan),
+        functools.partial(settle_kernel, plan),
         grid_spec=pltpu.PrefetchScalarGridSpec(
-            num_scalar_prefetch=2, grid=(seqs,),
-            in_specs=[
-                pl.BlockSpec((1, count, width_p, width_n), lambda s, *_: (s, 0, 0, 0)),
-                pl.BlockSpec((steps, count), lambda s, *_: (s, 0)),
-                pl.BlockSpec((slots, steps, width_n), lambda s, *_: (0, s, 0)),
-                pl.BlockSpec((steps, width_n), lambda s, *_: (s, 0)),
-                pl.BlockSpec((steps, width_n), lambda s, *_: (s, 0)),
-                pl.BlockSpec((steps, slots * width_p), lambda s, *_: (s, 0)),
-                pl.BlockSpec((steps, own * width_p), lambda s, *_: (s, 0)),
-                pl.BlockSpec((1, width_p, width_n), lambda s, *_: (s, 0, 0)),
-            ],
-            out_specs=[
-                pl.BlockSpec((1, count, width_p, width_n), lambda s, *_: (s, 0, 0, 0)),
-                pl.BlockSpec((steps, own * width_p), lambda s, *_: (s, 0)),
+            num_scalar_prefetch=2, grid=(1,),
+            in_specs=settled + [hbm],
+            out_specs=[hbm, whole((rows, own * width_p))],
+            scratch_shapes=[
+                pltpu.VMEM(low.shape, f32), pltpu.VMEM(merged.shape, f32),
+                pltpu.SemaphoreType.DMA((seqs, own)), pltpu.SemaphoreType.DMA((seqs, slots)),
             ],
         ),
         out_shape=[
             jax.ShapeDtypeStruct(states.shape, f32),
             jax.ShapeDtypeStruct((rows, own * width_p), f32),
         ],
+        input_output_aliases={2 + len(settled): 0},
         compiler_params=pltpu.CompilerParams(vmem_limit_bytes=VMEM),
-        cost_estimate=pl.CostEstimate(flops=20_000_000, bytes_accessed=32_000_000, transcendentals=0),
-        name="commit",
-    )(positions, accepted, states, factor, taken, in_vecs, out_vecs, token, draft, fold_in)
-    outputs = pl.pallas_call(
-        functools.partial(finish_kernel, plan),
+        cost_estimate=pl.CostEstimate(flops=8_000_000, bytes_accessed=8_000_000, transcendentals=0),
+        name="settle",
+    )(positions, accepted, sums, low, merged, taken, in_vecs, out_vecs, token, draft, fold_in, base_states)
+    outputs, share = pl.pallas_call(
+        functools.partial(finish_kernel, plan, 1.0 / (groups * seqs * steps)),
         grid=(1,),
-        in_specs=[whole((rows, own * width_p)), whole((rows, width_p))],
-        out_specs=whole((seqs, steps, own * width_p)),
-        out_shape=jax.ShapeDtypeStruct((seqs, steps, own * width_p), jnp.bfloat16),
+        in_specs=[whole((rows, own * width_p)), whole((rows, width_p)), whole(counted.shape), whole(counted.shape)],
+        out_specs=[whole((seqs, steps, own * width_p)), whole((1, 1))],
+        out_shape=[jax.ShapeDtypeStruct((seqs, steps, own * width_p), jnp.bfloat16),
+                   jax.ShapeDtypeStruct((1, 1), f32)],
+        compiler_params=pltpu.CompilerParams(vmem_limit_bytes=VMEM),
         name="finish",
-    )(own_out, received)
-    counted = summed_over(counted, "seq")
-    acceptance = counted[0, 0] / (lax.axis_size("seq") * seqs * steps)
-    return outputs, new_states, acceptance
+    )(own_out, received, summed, summed_in)
+    return outputs, new_states, share.reshape(())
 
 
 def dispatch(states, xbc, rates, level_weights, positions, accepted):
     plan = Plan(lax.axis_size("level"), states, xbc, rates)
-    step = functools.partial(fast_on_device, plan) if plan.fits() else on_device
+    step = functools.partial(fast_on_device, plan) if plan.fits(lax.axis_size("seq")) else on_device
     return step(states, xbc, rates, level_weights, positions, accepted)
 
 

time: 52.8 us -> 39.4 us (0.75)
  local copies, waits for them, and re-layouts: 10 us -> 0.01 us
  Pallas kernels: 18.1 us -> 26.2 us
  waiting for transfers between devices: 7.9 us -> 0.02 us
  between operations: 2.49 us -> 0.75 us
  starting transfers between devices: 13.8 us -> 12.1 us
    unnamed x22 -> x6, local copies, waits for them, and re-layouts: 9.53 us -> 0.01 us
    pallas_call x3 -> x4, Pallas kernels: 16.6 us -> 24.9 us  [the longest x1 16 us: fast_on_device(): pl.pallas_call(functools.partial(base_kernel, plan), grid_spec=pltpu.Pref...]
    ppermute x4, waiting for transfers between devices: 4.61 us -> 0.01 us  [fast_on_device(): lax.ppermute(x, 'level', [(i, i ^ by) for i in range(devices)])]
    ppermute x2, waiting for transfers between devices: 3.29 us -> 0.01 us  [fast_on_device(): lax.ppermute(x, 'seq', [(i, i ^ by) for i in range(groups)])]
    ppermute x2, starting transfers between devices: 4.49 us -> 2.75 us  [passed_along(): lax.ppermute(x, axis, [(i, (i + by) % devices) for i in range(devices)])]
  transfers between devices with their start and end apart: 8 -> 8, of which waited for: 4 -> 0; matrix products, arithmetic and copies ran while one was open for 1% -> 0% of each run, Pallas kernels for 32% -> 65%
where the time goes in v2:
time: 39.4 us; the launch traced here: 39.1 us
  Pallas kernels  26.2 us (66%)
  starting transfers between devices  12.1 us (31%)
  between operations  0.75 us (2%)
    pallas_call x1, Pallas kernels, fast_on_device(): pl.pallas_call(functools.partial(base_kernel, plan), grid_spec=pltpu.Pref...  16 us
    ppermute x4, starting transfers between devices, fast_on_device(): lax.ppermute(x, 'level', [(i, i ^ by) for i in range(devices)])  7.84 us
    pallas_call x1, Pallas kernels, fast_on_device(): pl.pallas_call(functools.partial(settle_kernel, plan), grid_spec=pltpu.Pr...  5.86 us
    ppermute x2, starting transfers between devices, passed_along(): lax.ppermute(x, axis, [(i, (i + by) % devices) for i in range(devices)])  2.75 us
    pallas_call x1, Pallas kernels, fast_on_device(): pl.pallas_call(functools.partial(tables_kernel, plan), grid=(1,), in_spec...  2.5 us
    ppermute x2, starting transfers between devices, fast_on_device(): lax.ppermute(x, 'seq', [(i, i ^ by) for i in range(groups)])  1.49 us
    pallas_call x1, Pallas kernels, fast_on_device(): pl.pallas_call(functools.partial(assemble_kernel, plan), grid=(1,), in_sp...  1.26 us
  transfers between devices with their start and end apart: 8, of which 0 were waited for; matrix products, arithmetic and copies ran while one was open for 0% of the time, Pallas kernels for 65%

profile of v2, /device:TPU:0, one launch (start us, length us, event | category | flops | bytes accessed | tf_op | source)
XLA Modules:
  0.0 39.1 jit_solution(6055842930052012186)
XLA Ops:
  0.6 0.0 copy-start.2
  0.6 0.0 copy-start.1
  0.7 0.0 copy-start
  0.7 3.1 %collective-permute-start = (bf16[8,8,224]{2,1,0:T(8,128)(2,1)}, bf16[8,8,224]{2,1,0:T(8,128)(2,1)S(1)}, u32[]{:S(2)}, u32[]{:S(2)}) collective-permute-start(bf16[8,8,224]{2,1,0:T(8,128)(2,1)} %param.7), channel_id=1, source_target_pairs={{0,1},{1,0},{2,3},{3,2},{4,5},{5,4},{6,7},{7,6},{8,9},{9,8},{10,11... | collective-permute-start | bytes 86024 | tf_op jit(solution)/shard_map/ppermute | solution.py:502
  3.7 2.5 %tables.1 = (f32[64,60]{1,0:T(8,128)S(1)}, f32[4,64,128]{2,1,0:T(8,128)S(1)}, f32[4,64,64]{2,1,0:T(8,128)S(1)}, f32[3,64,64]{2,1,0:T(8,128)S(1)}, bf16[8,64,128]{2,1,0:T(8,128)(2,1)S(1)}, /*index=5*/f32[8,128]{1,0:T(8,128)S(1)}) custom-call(s32[8]{0:T(128)} %pos.3, s32[8]{0:T(128)} %acc.3, f32[8,8,24]{2,1,0:T(8,128)} %rates_hbm.1, f32[8,8,60]{2,1,0:T(8,128)} %weights_hbm.1, ...), custom_call_target="tpu_custom_call" | custom-call | flops 2000000 | bytes 3000000 | tf_op jit(solution)/shard_map/tables/pallas_call | solution.py:507
  6.2 0.1 collective-permute-start.5
  6.3 0.0 collective-permute-done
  6.3 0.0 copy-done.2
  6.3 4.1 %collective-permute-start.3 = (bf16[2,8,8,224]{3,2,1,0:T(8,128)(2,1)S(1)}, bf16[2,8,8,224]{3,2,1,0:T(8,128)(2,1)S(1)}, u32[]{:S(2)}, u32[]{:S(2)}) collective-permute-start(bf16[2,8,8,224]{3,2,1,0:T(8,128)(2,1)S(1)} %pad_maximum_fusion.pair_ref), channel_id=1, source_target_pairs={{0,6},{1,7},{2,4},{3,5},{4,2},{5,3},{6,0},{7,1},{8,14},{9,15},{10,... | collective-permute-start | bytes 172040 | tf_op jit(solution)/shard_map/ppermute | solution.py:502
  10.5 0.0 collective-permute-start.2
  10.5 0.6 %collective-permute-start.1 = (bf16[2,8,8,224]{3,2,1,0:T(8,128)(2,1)S(1)}, bf16[2,8,8,224]{3,2,1,0:T(8,128)(2,1)S(1)}, u32[]{:S(2)}, u32[]{:S(2)}) collective-permute-start(bf16[2,8,8,224]{3,2,1,0:T(8,128)(2,1)S(1)} %pad_maximum_fusion.pair_ref), channel_id=1, source_target_pairs={{0,2},{1,3},{2,0},{3,1},{4,6},{5,7},{6,4},{7,5},{8,10},{9,11},{10,... | collective-permute-start | bytes 172040 | tf_op jit(solution)/shard_map/ppermute | solution.py:502
  11.1 0.0 collective-permute-start.4
  11.1 0.0 copy-done.1
  11.1 0.0 copy-done
  11.1 16.0 %base.1 = (f32[8,60,64,128]{3,2,1,0:T(8,128)}, f32[8,4,8,64,128]{4,3,2,1,0:T(8,128)S(1)}, f32[8,3,3,64,128]{4,3,2,1,0:T(8,128)S(1)}, f32[8,4,64,128]{3,2,1,0:T(8,128)S(1)}) custom-call(s32[8]{0:T(128)S(1)} %copy-done, s32[8]{0:T(128)S(1)} %copy-done.1, f32[8,60,64,128]{3,2,1,0:T(8,128)} %refs_5_.1, f32[8,60,64,128]{3,2,1,0:T(8,128)} %refs_5_.1, ...), custom_call_target="tpu_custom_call" | custom-call | flops 20000000 | bytes 32000000 | tf_op jit(solution)/shard_map/base/pallas_call | solution.py:532
  27.1 0.0 collective-permute-done.4.refs_7_
  27.1 0.0 collective-permute-done.3.refs_2_
  27.1 0.0 collective-permute-done.2.refs_1_
  27.1 0.0 collective-permute-done.1.refs_0_
  27.1 1.3 %assemble.1 = (f32[64,128]{1,0:T(8,128)S(1)}, f32[64,128]{1,0:T(8,128)S(1)}, f32[64,256]{1,0:T(8,128)S(1)}, f32[64,192]{1,0:T(8,128)S(1)}, f32[64,64]{1,0:T(8,128)S(1)}, /*index=5*/f32[8,128]{1,0:T(8,128)S(1)}) custom-call(bf16[2,8,8,224]{3,2,1,0:T(8,128)(2,1)S(1)} %pad_maximum_fusion.pair_ref, bf16[2,8,8,224]{3,2,1,0:T(8,128)(2,1)S(1)} %collective-permute-done.1.refs_0_, ...), custom_call_target="tpu_custom_call" | custom-call | flops 2000000 | bytes 3000000 | tf_op jit(solution)/shard_map/assemble/pallas_call | solution.py:567
  28.4 2.7 %collective-permute-start.6 = (f32[64,64]{1,0:T(8,128)S(1)}, f32[64,64]{1,0:T(8,128)S(1)}, u32[]{:S(2)}, u32[]{:S(2)}) collective-permute-start(f32[64,64]{1,0:T(8,128)S(1)} %get-tuple-element.38), channel_id=1, source_target_pairs={{0,1},{1,2},{2,3},{3,4},{4,5},{5,6},{6,7},{7,0},{8,9},{9,10},{10,1... | collective-permute-start | bytes 49160 | tf_op jit(solution)/shard_map/ppermute | solution.py:22
  31.1 1.5 %collective-permute-start.7 = (f32[8,128]{1,0:T(8,128)S(1)}, f32[8,128]{1,0:T(8,128)S(1)}, u32[]{:S(2)}, u32[]{:S(2)}) collective-permute-start(f32[8,128]{1,0:T(8,128)S(1)} %get-tuple-element.39.count_ref), channel_id=1, source_target_pairs={{0,16},{8,24},{16,0},{24,8},{1,17},{9,25},{17,1},{25,9},{2,18},{10... | collective-permute-start | bytes 12296 | tf_op jit(solution)/shard_map/ppermute | solution.py:565
  32.6 0.0 collective-permute-done.5.fold_ref
  32.6 5.9 %settle.1 = (f32[8,60,64,128]{3,2,1,0:T(8,128)}, f32[64,192]{1,0:T(8,128)S(1)}) custom-call(s32[8]{0:T(128)S(1)} %copy-done, s32[8]{0:T(128)S(1)} %copy-done.1, f32[8,4,8,64,128]{4,3,2,1,0:T(8,128)S(1)} %get-tuple-element.25.refs_3_.sums_ref, f32[8,3,3,64,128]{4,3,2,1,0:T(8,128)S(1)} %get-tuple-element.26.low_ref, ...), custom_call_target="tpu_custom_call", output_to_operand_aliasing={{0}: (11, {})} | custom-call | flops 8000000 | bytes 8000000 | tf_op jit(solution)/shard_map/settle/pallas_call | solution.py:593
  38.5 0.0 collective-permute-done.7.counted_ref
  38.5 0.0 collective-permute-done.6.received_ref
  38.5 0.6 %finish.1 = (bf16[8,8,192]{2,1,0:T(8,128)(2,1)}, f32[1,1]{1,0:T(1,128)}) custom-call(f32[64,192]{1,0:T(8,128)S(1)} %get-tuple-element.37.own_ref, f32[64,64]{1,0:T(8,128)S(1)} %collective-permute-done.6.received_ref, f32[8,128]{1,0:T(8,128)S(1)} %get-tuple-element.39.count_ref, f32[8,128]{1,0:T(8,128)S(1)} %collective-permute-done.7.counted_ref), custom_call_target="tpu_custom_call" | custom-call | tf_op jit(solution)/shard_map/finish/pallas_call | solution.py:613
  (1 shorter events, 0.0 us)
Async XLA Ops:
  0.6 5.7 %copy-start.2 = (bf16[8,8,224]{2,1,0:T(8,128)(2,1)S(1)}, bf16[8,8,224]{2,1,0:T(8,128)(2,1)}, u32[]{:S(2)}) copy-start(bf16[8,8,224]{2,1,0:T(8,128)(2,1)} %param.7) | copy-start | bytes 86020
  0.6 10.5 %copy-start.1 = (s32[8]{0:T(128)S(1)}, s32[8]{0:T(128)}, u32[]{:S(2)}) copy-start(s32[8]{0:T(128)} %acc.3) | copy-start | bytes 100
  0.7 10.5 %copy-start = (s32[8]{0:T(128)S(1)}, s32[8]{0:T(128)}, u32[]{:S(2)}) copy-start(s32[8]{0:T(128)} %pos.3) | copy-start | bytes 100
  0.7 5.6 %collective-permute-start = (bf16[8,8,224]{2,1,0:T(8,128)(2,1)}, bf16[8,8,224]{2,1,0:T(8,128)(2,1)S(1)}, u32[]{:S(2)}, u32[]{:S(2)}) collective-permute-start(bf16[8,8,224]{2,1,0:T(8,128)(2,1)} %param.7), channel_id=1, source_target_pairs={{0,1},{1,0},{2,3},{3,2},{4,5},{5,4},{6,7},{7,6},{8,9},{9,8},{10,11... | collective-permute-start | bytes 86024 | tf_op jit(solution)/shard_map/ppermute | solution.py:502
  6.2 26.4 %collective-permute-start.5 = (bf16[8,64,128]{2,1,0:T(8,128)(2,1)S(1)}, bf16[8,64,128]{2,1,0:T(8,128)(2,1)S(1)}, u32[]{:S(2)}, u32[]{:S(2)}) collective-permute-start(bf16[8,64,128]{2,1,0:T(8,128)(2,1)S(1)} %get-tuple-element.35), channel_id=1, source_target_pairs={{0,1},{1,2},{2,3},{3,4},{4,5},{5,6},{6,7},{7,0},{8,9},{9,10},{10,1... | collective-permute-start | bytes 393224 | tf_op jit(solution)/shard_map/ppermute | solution.py:22
  6.3 20.8 %collective-permute-start.3 = (bf16[2,8,8,224]{3,2,1,0:T(8,128)(2,1)S(1)}, bf16[2,8,8,224]{3,2,1,0:T(8,128)(2,1)S(1)}, u32[]{:S(2)}, u32[]{:S(2)}) collective-permute-start(bf16[2,8,8,224]{3,2,1,0:T(8,128)(2,1)S(1)} %pad_maximum_fusion.pair_ref), channel_id=1, source_target_pairs={{0,6},{1,7},{2,4},{3,5},{4,2},{5,3},{6,0},{7,1},{8,14},{9,15},{10,... | collective-permute-start | bytes 172040 | tf_op jit(solution)/shard_map/ppermute | solution.py:502
  10.5 16.6 %collective-permute-start.2 = (bf16[2,8,8,224]{3,2,1,0:T(8,128)(2,1)S(1)}, bf16[2,8,8,224]{3,2,1,0:T(8,128)(2,1)S(1)}, u32[]{:S(2)}, u32[]{:S(2)}) collective-permute-start(bf16[2,8,8,224]{3,2,1,0:T(8,128)(2,1)S(1)} %pad_maximum_fusion.pair_ref), channel_id=1, source_target_pairs={{0,4},{1,5},{2,6},{3,7},{4,0},{5,1},{6,2},{7,3},{8,12},{9,13},{10,... | collective-permute-start | bytes 172040 | tf_op jit(solution)/shard_map/ppermute | solution.py:502
  10.5 16.6 %collective-permute-start.1 = (bf16[2,8,8,224]{3,2,1,0:T(8,128)(2,1)S(1)}, bf16[2,8,8,224]{3,2,1,0:T(8,128)(2,1)S(1)}, u32[]{:S(2)}, u32[]{:S(2)}) collective-permute-start(bf16[2,8,8,224]{3,2,1,0:T(8,128)(2,1)S(1)} %pad_maximum_fusion.pair_ref), channel_id=1, source_target_pairs={{0,2},{1,3},{2,0},{3,1},{4,6},{5,7},{6,4},{7,5},{8,10},{9,11},{10,... | collective-permute-start | bytes 172040 | tf_op jit(solution)/shard_map/ppermute | solution.py:502
  11.1 16.0 %collective-permute-start.4 = (f32[8,128]{1,0:T(8,128)S(1)}, f32[8,128]{1,0:T(8,128)S(1)}, u32[]{:S(2)}, u32[]{:S(2)}) collective-permute-start(f32[8,128]{1,0:T(8,128)S(1)} %get-tuple-element.30.refs_6_), channel_id=1, source_target_pairs={{0,8},{8,0},{16,24},{24,16},{1,9},{9,1},{17,25},{25,17},{2,10},{10... | collective-permute-start | bytes 12296 | tf_op jit(solution)/shard_map/ppermute | solution.py:565
  28.4 10.1 %collective-permute-start.6 = (f32[64,64]{1,0:T(8,128)S(1)}, f32[64,64]{1,0:T(8,128)S(1)}, u32[]{:S(2)}, u32[]{:S(2)}) collective-permute-start(f32[64,64]{1,0:T(8,128)S(1)} %get-tuple-element.38), channel_id=1, source_target_pairs={{0,1},{1,2},{2,3},{3,4},{4,5},{5,6},{6,7},{7,0},{8,9},{9,10},{10,1... | collective-permute-start | bytes 49160 | tf_op jit(solution)/shard_map/ppermute | solution.py:22
  31.1 7.4 %collective-permute-start.7 = (f32[8,128]{1,0:T(8,128)S(1)}, f32[8,128]{1,0:T(8,128)S(1)}, u32[]{:S(2)}, u32[]{:S(2)}) collective-permute-start(f32[8,128]{1,0:T(8,128)S(1)} %get-tuple-element.39.count_ref), channel_id=1, source_target_pairs={{0,16},{8,24},{16,0},{24,8},{1,17},{9,25},{17,1},{25,9},{2,18},{10... | collective-permute-start | bytes 12296 | tf_op jit(solution)/shard_map/ppermute | solution.py:565
